TPU v7x, 512 devices: a whole 4x4x16 slice. The times are simulated.
512 devices in a mesh: rows: 32 (over x, z_lo), cols: 16 (over z_hi, y, core).
Axes of the slice: x: 4, y: 4, z: 16 (z_hi: 2, z_lo: 8; z = z_hi * 8 + z_lo), core: 2. Of those that a mesh axis runs over, the one named last changes fastest.
Arguments:
- image_in: bfloat16 [1, 512, 1536, 256], P(None, 'rows', 'cols'), may hold values from -6 to 6
- cotangent: bfloat16 [1, 512, 1536, 256], P(None, 'rows', 'cols'), may hold values from -6 to 6
- first_kernel: bfloat16 [3, 3, 256, 256], replicated, may hold values from -0.125 to 0.125
- first_bias: float32 [256], replicated, may hold values from -3 to 3
- second_kernel: bfloat16 [3, 3, 256, 256], replicated, may hold values from -0.125 to 0.125
- first_center: float32 [32], replicated, may hold values from -3 to 3
- first_inverse: float32 [32], replicated, may hold values from 0.5 to 2
- first_gain: float32 [256], replicated, may hold values from 0.5 to 1.5
- first_shift: float32 [256], replicated, may hold values from -3 to 3
- second_center: float32 [32], replicated, may hold values from -3 to 3
- second_inverse: float32 [32], replicated, may hold values from 0.5 to 2
- second_gain: float32 [256], replicated, may hold values from 0.5 to 1.5
- second_shift: float32 [256], replicated, may hold values from -3 to 3
Outputs:
- image_grad: bfloat16 [1, 512, 1536, 256], P(None, 'rows', 'cols')
All inputs are finite; a program needn't handle non-finite values.
Results may differ from a plain program's by a relative error of at most 0.0044.
Values may be sent and summed in bfloat16 or wider, within the bound.
No kernel may reach another device: no remote copies, remote signals or barrier semaphores. Data moves between devices by JAX's collectives and lax.ppermute only.
A program may use at most 64 MiB of HBM per device.

v0:
```python
import jax
import jax.numpy as jnp
from jax import lax
from jax.sharding import PartitionSpec as P


def with_halo(x, sides, width):
    for axis, dim in sides:
        size, length = (lax.axis_size(axis), x.shape[dim])
        up = [(i, (i + 1) % size) for i in range(size - 1)]
        down = [(j, i) for i, j in up]
        last = lax.slice_in_dim(x, length - width, length, axis=dim)
        leading = lax.slice_in_dim(x, 0, width, axis=dim)
        before = lax.ppermute(last, axis, up)
        after = lax.ppermute(leading, axis, down)
        x = jnp.concatenate([before, x, after], axis=dim)
    return x


def silu_slope(value):
    sig = jax.nn.sigmoid(value)
    return sig * (1.0 + value * (1.0 - sig))


def convolve(field, kernel):
    return lax.conv_general_dilated(
        field,
        kernel,
        (1, 1),
        "VALID",
        dimension_numbers=("NHWC", "HWIO", "NHWC"),
        preferred_element_type=jnp.float32,
    )


def flipped(kernel):
    return jnp.transpose(kernel[::-1, ::-1], (0, 1, 3, 2))


def inside_mask(tile_rows, tile_cols, margin):
    row_pos = (
        lax.axis_index("rows") * tile_rows
        + jnp.arange(tile_rows + 2 * margin, dtype=jnp.int32)
        - margin
    )
    col_pos = (
        lax.axis_index("cols") * tile_cols
        + jnp.arange(tile_cols + 2 * margin, dtype=jnp.int32)
        - margin
    )
    row_ok = (row_pos >= 0) & (row_pos < tile_rows * lax.axis_size("rows"))
    col_ok = (col_pos >= 0) & (col_pos < tile_cols * lax.axis_size("cols"))
    return (row_ok[:, None] & col_ok[None, :]).astype(jnp.float32)[:, :, None]


def per_device(
    image_in,
    cotangent,
    first_kernel,
    first_bias,
    second_kernel,
    first_center,
    first_inverse,
    first_gain,
    first_shift,
    second_center,
    second_inverse,
    second_gain,
    second_shift,
):
    tile_rows = image_in.shape[1]
    tile_cols = image_in.shape[2]
    repeats = image_in.shape[3] // first_center.shape[0]
    center_one = jnp.repeat(first_center, repeats)
    center_two = jnp.repeat(second_center, repeats)
    scale_one = jnp.repeat(first_inverse, repeats) * first_gain
    scale_two = jnp.repeat(second_inverse, repeats) * second_gain
    kernel_back_two = flipped(second_kernel)
    kernel_back_one = flipped(first_kernel)
    pre_one = (image_in.astype(jnp.float32) - center_one) * scale_one + first_shift
    stacked = jnp.stack((image_in, cotangent))
    widened = with_halo(stacked, (("rows", 2), ("cols", 3)), 2)
    pre_wide = (widened[0].astype(jnp.float32) - center_one) * scale_one + first_shift
    act_wide = (jax.nn.silu(pre_wide) * inside_mask(tile_rows, tile_cols, 2)).astype(jnp.bfloat16)
    pre_two = (
        convolve(act_wide, first_kernel) + first_bias - center_two
    ) * scale_two + second_shift
    back_two = convolve(widened[1], kernel_back_two)
    inner_wide = back_two * silu_slope(pre_two) * scale_two
    inner_padded = (inner_wide * inside_mask(tile_rows, tile_cols, 1)).astype(jnp.bfloat16)
    back_one = convolve(inner_padded, kernel_back_one)
    result = cotangent.astype(jnp.float32) + back_one * silu_slope(pre_one) * scale_one
    return result.astype(jnp.bfloat16)


def solution(mesh):
    return jax.shard_map(
        per_device,
        mesh=mesh,
        in_specs=(
            P(None, "rows", "cols", None),
            P(None, "rows", "cols", None),
            P(),
            P(),
            P(),
            P(),
            P(),
            P(),
            P(),
            P(),
            P(),
            P(),
            P(),
        ),
        out_specs=P(None, "rows", "cols", None),
        check_vma=False,
    )
```

profile of v0, /device:TPU:29, one launch (start us, length us, event | category | flops | bytes accessed | tf_op | source)
XLA Modules:
  0.0 88.2 jit_solution(11199919267853296757)
XLA Ops:
  0.0 1.2 %pad_maximum_fusion.2 = (bf16[2,1,2,96,256]{4,3,2,1,0:T(8,128)(2,1)S(1)}, bf16[2,1,2,96,256]{4,3,2,1,0:T(8,128)(2,1)S(1)}) fusion(bf16[1,1,16,96,256]{4,3,2,1,0:T(8,128)(2,1)} %bitcast.46, bf16[1,1,16,96,256]{4,3,2,1,0:T(8,128)(2,1)} %bitcast.49), kind=kLoop, calls=%fused_computation.48 | loop fusion | flops 196608 | bytes 1966080 | tf_op jit(solution)/shard_map/slice | solution.py:12
  1.2 3.5 %collective-permute-start = (bf16[2,1,2,96,256]{4,3,2,1,0:T(8,128)(2,1)S(1)}, bf16[2,1,2,96,256]{4,3,2,1,0:T(8,128)(2,1)S(1)}, u32[]{:S(2)}, u32[]{:S(2)}) collective-permute-start(bf16[2,1,2,96,256]{4,3,2,1,0:T(8,128)(2,1)S(1)} %get-tuple-element.7), channel_id=1, source_target_pairs={{0,16},{16,32},{32,48},{48,64},{64,80},{80,96},{96,112},{112,128},... | collective-permute-start | bytes 589832 | tf_op jit(solution)/shard_map/ppermute | solution.py:14
  4.8 11.2 %collective-permute-start.1 = (bf16[2,1,2,96,256]{4,3,2,1,0:T(8,128)(2,1)S(1)}, bf16[2,1,2,96,256]{4,3,2,1,0:T(8,128)(2,1)S(1)}, u32[]{:S(2)}, u32[]{:S(2)}) collective-permute-start(bf16[2,1,2,96,256]{4,3,2,1,0:T(8,128)(2,1)S(1)} %get-tuple-element.8), channel_id=1, source_target_pairs={{16,0},{32,16},{48,32},{64,48},{80,64},{96,80},{112,96},{128,112},... | collective-permute-start | bytes 589832 | tf_op jit(solution)/shard_map/ppermute | solution.py:15
  16.0 0.6 compare_and_fusion.1
  16.6 0.5 compare_and_fusion.3
  17.2 0.7 and_convert_fusion.1
  17.9 0.8 collective-permute-done
  18.7 0.9 %collective-permute-done.1 = bf16[2,1,2,96,256]{4,3,2,1,0:T(8,128)(2,1)S(1)} collective-permute-done((bf16[2,1,2,96,256]{4,3,2,1,0:T(8,128)(2,1)S(1)}, bf16[2,1,2,96,256]{4,3,2,1,0:T(8,128)(2,1)S(1)}, u32[]{:S(2)}, u32[]{:S(2)}) %collective-permute-start.1) | collective-permute-done | bytes 196640 | tf_op jit(solution)/shard_map/ppermute | solution.py:15
  19.6 0.1 pad_maximum_fusion.6
  19.7 14.5 %collective-permute-start.2 = (bf16[2,1,20,2,256]{4,3,2,1,0:T(2,128)(2,1)S(1)}, bf16[2,1,20,2,256]{4,3,2,1,0:T(2,128)(2,1)S(1)}, u32[]{:S(2)}, u32[]{:S(2)}) collective-permute-start(bf16[2,1,20,2,256]{4,3,2,1,0:T(2,128)(2,1)S(1)} %get-tuple-element.5), channel_id=1, source_target_pairs={{0,1},{1,2},{2,3},{3,4},{4,5},{5,6},{6,7},{7,8},{8,9},{9,10},{10,1... | collective-permute-start | bytes 122888 | tf_op jit(solution)/shard_map/ppermute | solution.py:14
  34.2 1.9 %collective-permute-start.3 = (bf16[2,1,20,2,256]{4,3,2,1,0:T(2,128)(2,1)S(1)}, bf16[2,1,20,2,256]{4,3,2,1,0:T(2,128)(2,1)S(1)}, u32[]{:S(2)}, u32[]{:S(2)}) collective-permute-start(bf16[2,1,20,2,256]{4,3,2,1,0:T(2,128)(2,1)S(1)} %get-tuple-element.6), channel_id=1, source_target_pairs={{1,0},{2,1},{3,2},{4,3},{5,4},{6,5},{7,6},{8,7},{9,8},{10,9},{11,1... | collective-permute-start | bytes 122888 | tf_op jit(solution)/shard_map/ppermute | solution.py:15
  36.2 0.1 and_convert_fusion
  36.2 0.7 broadcast_in_dim.8
  37.0 0.1 sub.56
  37.0 0.7 broadcast_in_dim.9
  37.8 0.1 reshape.187
  37.9 0.7 broadcast_in_dim.10
  38.6 0.1 sub.61
  38.7 0.7 broadcast_in_dim.11
  39.4 0.1 reshape.188
  39.5 0.7 mul.120
  40.2 10.1 %collective-permute-done.3 = bf16[2,1,20,2,256]{4,3,2,1,0:T(2,128)(2,1)S(1)} collective-permute-done((bf16[2,1,20,2,256]{4,3,2,1,0:T(2,128)(2,1)S(1)}, bf16[2,1,20,2,256]{4,3,2,1,0:T(2,128)(2,1)S(1)}, u32[]{:S(2)}, u32[]{:S(2)}) %collective-permute-start.3) | collective-permute-done | bytes 40992 | tf_op jit(solution)/shard_map/ppermute | solution.py:15
  50.4 1.2 %pad_maximum_fusion = bf16[2,1,20,100,256]{4,3,2,1,0:T(8,128)(2,1)S(1)} fusion(bf16[2,1,20,2,256]{4,3,2,1,0:T(2,128)(2,1)S(1)} %collective-permute-done.3, bf16[2,1,2,96,256]{4,3,2,1,0:T(8,128)(2,1)S(1)} %collective-permute-done.1, bf16[1,1,16,96,256]{4,3,2,1,0:T(8,128)(2,1)S(1)} %bitcast.48, bf16[1,1,16,96,256]{4,3,2,1,0:T(8,128)(2,1)S(1)} %bitcast.51, ...), kind=kLoop, calls=%fused_computation.5 | loop fusion | flops 12288000 | bytes 4096000 | tf_op jit(solution)/shard_map/concatenate | solution.py:16
  51.5 0.0 copy-start.5
  51.5 0.1 slice_bitcast_fusion.2
  51.6 1.0 %pad = bf16[20,1,104,256]{3,2,0,1:T(8,128)(2,1)} pad(bf16[20,1,100,256]{3,2,0,1:T(8,128)(2,1)S(1)} %slice_bitcast_fusion.2, bf16[]{:T(256)} %constant.41), padding=0_0x0_0x0_4x0_0 | pad | bytes 2088962 | tf_op jit(solution)/shard_map/squeeze | solution.py:88
  52.7 0.7 fusion.36
  53.4 1.1 %pad.2 = bf16[20,1,104,256]{3,2,0,1:T(8,128)(2,1)} pad(bf16[20,1,100,256]{3,2,0,1:T(8,128)(2,1)S(1)} %fusion.36, bf16[]{:T(256)} %constant.41), padding=0_0x0_0x0_4x0_0 | pad | bytes 2088962 | tf_op jit(solution)/shard_map/convert_element_type | solution.py:84
  54.5 2.9 %reshape.196 = bf16[20,1,8,13,256]{4,3,2,0,1:T(8,128)(2,1)} reshape(bf16[20,1,104,256]{3,2,0,1:T(8,128)(2,1)} %pad.2) | data formatting | bytes 2129920 | tf_op jit(solution)/shard_map/conv_general_dilated | solution.py:26
  57.4 1.8 %copy.18 = bf16[20,1,8,13,256]{4,2,3,0,1:T(8,128)(2,1)S(1)} copy(bf16[20,1,8,13,256]{4,3,2,0,1:T(8,128)(2,1)} %reshape.196) | data formatting | bytes 2129920 | tf_op jit(solution)/shard_map/conv_general_dilated | solution.py:26
  59.2 1.0 %copy-done.3 = bf16[20,1,8,13,256]{4,2,3,0,1:T(8,128)(2,1)} copy-done((bf16[20,1,8,13,256]{4,2,3,0,1:T(8,128)(2,1)}, bf16[20,1,8,13,256]{4,2,3,0,1:T(8,128)(2,1)S(1)}, u32[]{:S(2)}) %copy-start.3) | copy-done | bytes 1064984
  60.2 2.9 %reshape.191 = bf16[20,1,8,13,256]{4,3,2,0,1:T(8,128)(2,1)} reshape(bf16[20,1,104,256]{3,2,0,1:T(8,128)(2,1)} %pad) | data formatting | bytes 2129920 | tf_op jit(solution)/shard_map/conv_general_dilated | solution.py:26
  63.1 1.9 %copy.16 = bf16[20,1,8,13,256]{4,2,3,0,1:T(8,128)(2,1)S(1)} copy(bf16[20,1,8,13,256]{4,3,2,0,1:T(8,128)(2,1)} %reshape.191) | data formatting | bytes 2129920 | tf_op jit(solution)/shard_map/conv_general_dilated | solution.py:26
  65.1 0.0 copy-start.9
  65.1 0.0 copy-start.10
  65.1 0.0 copy-start.12
  65.1 2.6 %fusion.19 = f32[18,8,13,256]{3,1,2,0:T(8,128)S(1)} fusion(bf16[3,3,256,256]{3,2,1,0:T(8,128)(2,1)S(1)} %copy-done.8, bf16[20,1,7,2,256]{4,2,3,0,1:T(8,128)(2,1)S(1)} %slice.30, bf16[20,1,8,13,256]{4,2,3,0,1:T(8,128)(2,1)S(1)} %copy.16), kind=kOutput, calls=%fused_computation.27 | convolution fusion | flops 2211987456 | bytes 4304896 | tf_op jit(solution)/shard_map/conv_general_dilated | solution.py:26
  67.8 3.4 %multiply_multiply_fusion = f32[18,8,13,256]{3,1,2,0:T(8,128)S(1)} fusion(f32[18,8,13,256]{3,1,2,0:T(8,128)S(1)} %fusion.19, bf16[3,3,256,256]{3,2,1,0:T(8,128)(2,1)S(1)} %copy-done, bf16[20,1,7,2,256]{4,2,3,0,1:T(8,128)(2,1)S(1)} %slice.32, bf16[20,1,8,13,256]{4,2,3,0,1:T(8,128)(2,1)S(1)} %copy-done.4, f32[256]{0:T(256)S(1)} %copy-done.9, ...), kind=kOutput, calls=%fused_computation.18 | convolution fusion | flops 2219175936 | bytes 6226024 | tf_op jit(solution)/shard_map/conv_general_dilated | solution.py:26
  71.2 2.1 %copy.19 = f32[18,8,13,256]{3,2,1,0:T(8,128)} copy(f32[18,8,13,256]{3,1,2,0:T(8,128)S(1)} %multiply_multiply_fusion) | data formatting | bytes 3833856 | tf_op jit(solution)/shard_map/mul | solution.py:89
  73.3 2.7 %reshape.200 = f32[18,1,104,256]{3,2,0,1:T(8,128)} reshape(f32[18,8,13,256]{3,2,1,0:T(8,128)} %copy.19) | data formatting | bytes 3833856 | tf_op jit(solution)/shard_map/mul | solution.py:89
  76.0 1.8 %fusion.12 = bf16[18,1,98,256]{3,2,0,1:T(8,128)(2,1)S(1)} fusion(f32[18,1,104,256]{3,2,0,1:T(8,128)} %reshape.200, f32[18,98]{1,0:T(8,128)S(1)} %and_convert_fusion), kind=kLoop, calls=%fused_computation.17 | loop fusion | flops 903168 | bytes 2716560 | tf_op jit(solution)/shard_map/convert_element_type | solution.py:90
  77.8 1.0 %pad.4 = bf16[18,1,104,256]{3,2,0,1:T(8,128)(2,1)} pad(bf16[18,1,98,256]{3,2,0,1:T(8,128)(2,1)S(1)} %fusion.12, bf16[]{:T(256)} %constant.41), padding=0_0x0_0x0_6x0_0 | pad | bytes 1861634 | tf_op jit(solution)/shard_map/convert_element_type | solution.py:90
  78.8 2.3 %reshape.203 = bf16[18,1,8,13,256]{4,3,2,0,1:T(8,128)(2,1)} reshape(bf16[18,1,104,256]{3,2,0,1:T(8,128)(2,1)} %pad.4) | data formatting | bytes 1916928 | tf_op jit(solution)/shard_map/conv_general_dilated | solution.py:26
  81.1 1.7 %copy.21 = bf16[18,1,8,13,256]{4,2,3,0,1:T(8,128)(2,1)S(1)} copy(bf16[18,1,8,13,256]{4,3,2,0,1:T(8,128)(2,1)} %reshape.203) | data formatting | bytes 1916928 | tf_op jit(solution)/shard_map/conv_general_dilated | solution.py:26
  82.8 2.3 %convolution_select_fusion = f32[16,8,13,256]{3,1,2,0:T(8,128)S(1)} fusion(bf16[3,3,256,256]{3,2,1,0:T(8,128)(2,1)S(1)} %copy-done, bf16[18,1,7,2,256]{4,2,3,0,1:T(8,128)(2,1)S(1)} %slice.34, bf16[18,1,8,13,256]{4,2,3,0,1:T(8,128)(2,1)S(1)} %copy.21, pred[8,13]{0,1:T(8,128)(4,1)S(1)} %copy-done.11), kind=kOutput, calls=%fused_computation.24 | convolution fusion | flops 1966678016 | bytes 3971176 | tf_op jit(solution)/shard_map/conv_general_dilated | solution.py:26
  85.2 0.6 copy.22
  85.7 1.3 %fusion.16 = bf16[1,16,96,256]{3,1,2,0:T(8,128)(2,1)S(1)} fusion(f32[16,1,104,256]{3,0,2,1:T(8,128)S(1)} %bitcast.52, bf16[1,16,96,256]{3,2,1,0:T(8,128)(2,1)S(1)} %copy-done.2, bf16[1,16,96,256]{3,2,1,0:T(8,128)(2,1)S(1)} %copy-done.1, f32[256]{0:T(256)S(1)} %copy-done.5, f32[256]{0:T(256)S(1)} %mul.112, f32[256]{0:T(256)S(1)} %sub.56), kind=kLoop, calls=%fused_computation.23 | loop fusion | flops 6291456 | bytes 3935232 | tf_op jit(solution)/shard_map/convert_element_type | solution.py:93
  87.1 1.1 %copy.24 = bf16[1,16,96,256]{3,2,1,0:T(8,128)(2,1)} copy(bf16[1,16,96,256]{3,1,2,0:T(8,128)(2,1)S(1)} %fusion.16) | data formatting | bytes 1572864 | tf_op jit(solution)/shard_map/convert_element_type | solution.py:93
  (28 shorter events, 0.2 us)
Async XLA Ops:
  0.0 67.7 %copy-start = (bf16[3,3,256,256]{3,2,1,0:T(8,128)(2,1)S(1)}, bf16[3,3,256,256]{3,2,1,0:T(8,128)(2,1)}, u32[]{:S(2)}) copy-start(bf16[3,3,256,256]{3,2,1,0:T(8,128)(2,1)} %param.15) | copy-start | bytes 3538948
  0.0 19.6 %copy-start.1 = (bf16[1,16,96,256]{3,2,1,0:T(8,128)(2,1)S(1)}, bf16[1,16,96,256]{3,2,1,0:T(8,128)(2,1)}, u32[]{:S(2)}) copy-start(bf16[1,16,96,256]{3,2,1,0:T(8,128)(2,1)} %param.14) | copy-start | bytes 2359300
  0.0 19.6 %copy-start.2 = (bf16[1,16,96,256]{3,2,1,0:T(8,128)(2,1)S(1)}, bf16[1,16,96,256]{3,2,1,0:T(8,128)(2,1)}, u32[]{:S(2)}) copy-start(bf16[1,16,96,256]{3,2,1,0:T(8,128)(2,1)} %param.13) | copy-start | bytes 2359300
  0.0 39.5 %copy-start.6 = (f32[256]{0:T(256)S(1)}, f32[256]{0:T(256)}, u32[]{:S(2)}) copy-start(f32[256]{0:T(256)} %param.20) | copy-start | bytes 3076
  1.2 17.4 %collective-permute-start = (bf16[2,1,2,96,256]{4,3,2,1,0:T(8,128)(2,1)S(1)}, bf16[2,1,2,96,256]{4,3,2,1,0:T(8,128)(2,1)S(1)}, u32[]{:S(2)}, u32[]{:S(2)}) collective-permute-start(bf16[2,1,2,96,256]{4,3,2,1,0:T(8,128)(2,1)S(1)} %get-tuple-element.7), channel_id=1, source_target_pairs={{0,16},{16,32},{32,48},{48,64},{64,80},{80,96},{96,112},{112,128},... | collective-permute-start | bytes 589832 | tf_op jit(solution)/shard_map/ppermute | solution.py:14
  4.8 14.8 %collective-permute-start.1 = (bf16[2,1,2,96,256]{4,3,2,1,0:T(8,128)(2,1)S(1)}, bf16[2,1,2,96,256]{4,3,2,1,0:T(8,128)(2,1)S(1)}, u32[]{:S(2)}, u32[]{:S(2)}) collective-permute-start(bf16[2,1,2,96,256]{4,3,2,1,0:T(8,128)(2,1)S(1)} %get-tuple-element.8), channel_id=1, source_target_pairs={{16,0},{32,16},{48,32},{64,48},{80,64},{96,80},{112,96},{128,112},... | collective-permute-start | bytes 589832 | tf_op jit(solution)/shard_map/ppermute | solution.py:15
  17.2 19.0 %copy-start.7 = (pred[18]{0:T(512)(128)(4,1)S(1)}, pred[18]{0:T(512)(128)(4,1)}, u32[]{:S(2)}) copy-start(pred[18]{0:T(512)(128)(4,1)} %compare_and_fusion.1) | copy-start | bytes 58
  19.7 20.5 %collective-permute-start.2 = (bf16[2,1,20,2,256]{4,3,2,1,0:T(2,128)(2,1)S(1)}, bf16[2,1,20,2,256]{4,3,2,1,0:T(2,128)(2,1)S(1)}, u32[]{:S(2)}, u32[]{:S(2)}) collective-permute-start(bf16[2,1,20,2,256]{4,3,2,1,0:T(2,128)(2,1)S(1)} %get-tuple-element.5), channel_id=1, source_target_pairs={{0,1},{1,2},{2,3},{3,4},{4,5},{5,6},{6,7},{7,8},{8,9},{9,10},{10,1... | collective-permute-start | bytes 122888 | tf_op jit(solution)/shard_map/ppermute | solution.py:14
  34.2 16.1 %collective-permute-start.3 = (bf16[2,1,20,2,256]{4,3,2,1,0:T(2,128)(2,1)S(1)}, bf16[2,1,20,2,256]{4,3,2,1,0:T(2,128)(2,1)S(1)}, u32[]{:S(2)}, u32[]{:S(2)}) collective-permute-start(bf16[2,1,20,2,256]{4,3,2,1,0:T(2,128)(2,1)S(1)} %get-tuple-element.6), channel_id=1, source_target_pairs={{1,0},{2,1},{3,2},{4,3},{5,4},{6,5},{7,6},{8,7},{9,8},{10,9},{11,1... | collective-permute-start | bytes 122888 | tf_op jit(solution)/shard_map/ppermute | solution.py:15
  51.5 1.1 %copy-start.5 = (f32[256]{0:T(256)S(1)}, f32[256]{0:T(256)}, u32[]{:S(2)}) copy-start(f32[256]{0:T(256)} %param.21) | copy-start | bytes 3076
  59.2 1.0 %copy-start.3 = (bf16[20,1,8,13,256]{4,2,3,0,1:T(8,128)(2,1)}, bf16[20,1,8,13,256]{4,2,3,0,1:T(8,128)(2,1)S(1)}, u32[]{:S(2)}) copy-start(bf16[20,1,8,13,256]{4,2,3,0,1:T(8,128)(2,1)S(1)} %copy.18) | copy-start | bytes 3194884
  63.1 1.9 %copy-start.8 = (bf16[3,3,256,256]{3,2,1,0:T(8,128)(2,1)S(1)}, bf16[3,3,256,256]{3,2,1,0:T(8,128)(2,1)}, u32[]{:S(2)}) copy-start(bf16[3,3,256,256]{3,2,1,0:T(8,128)(2,1)} %param.17) | copy-start | bytes 3538948
  65.0 2.7 %copy-start.4 = (bf16[20,1,8,13,256]{4,2,3,0,1:T(8,128)(2,1)S(1)}, bf16[20,1,8,13,256]{4,2,3,0,1:T(8,128)(2,1)}, u32[]{:S(2)}) copy-start(bf16[20,1,8,13,256]{4,2,3,0,1:T(8,128)(2,1)} %copy-done.3) | copy-start | bytes 3194884
  65.1 2.7 %copy-start.9 = (f32[256]{0:T(256)S(1)}, f32[256]{0:T(256)}, u32[]{:S(2)}) copy-start(f32[256]{0:T(256)} %param.25) | copy-start | bytes 3076
  65.1 2.7 %copy-start.10 = (f32[256]{0:T(256)S(1)}, f32[256]{0:T(256)}, u32[]{:S(2)}) copy-start(f32[256]{0:T(256)} %param.16) | copy-start | bytes 3076
  65.1 2.7 %copy-start.12 = (pred[8,13]{0,1:T(8,128)(4,1)S(1)}, pred[8,13]{0,1:T(8,128)(4,1)}, u32[]{:S(2)}) copy-start(pred[8,13]{0,1:T(8,128)(4,1)} %constant.54) | copy-start | bytes 316
  78.8 4.0 %copy-start.11 = (pred[8,13]{0,1:T(8,128)(4,1)S(1)}, pred[8,13]{0,1:T(8,128)(4,1)}, u32[]{:S(2)}) copy-start(pred[8,13]{0,1:T(8,128)(4,1)} %constant.53) | copy-start | bytes 316
where the time goes:
time: 88.7 us; the launch traced here: 88.2 us
  starting transfers between devices  31.2 us (35%)
  local copies, waits for them, and re-layouts  27.5 us (31%)
  waiting for transfers between devices  11.8 us (13%)
  other arithmetic  8.96 us (10%)
  matrix products  8.33 us (9%)
    ppermute x2, starting transfers between devices, with_halo(): before = lax.ppermute(last, axis, up)  18.1 us
    conv_general_dilated x10, local copies, waits for them, and re-layouts, convolve(): lax.conv_general_dilated(field, kernel, (1, 1), 'VALID', dimension_number...  14.1 us
    ppermute x2, starting transfers between devices, with_halo(): after = lax.ppermute(leading, axis, down)  13.1 us
    ppermute x2, waiting for transfers between devices, with_halo(): after = lax.ppermute(leading, axis, down)  11 us
    conv_general_dilated x3, matrix products, convolve(): lax.conv_general_dilated(field, kernel, (1, 1), 'VALID', dimension_number...  8.33 us
    mul x2, local copies, waits for them, and re-layouts, per_device(): inner_wide = back_two * silu_slope(pre_two) * scale_two  4.82 us
    convert_element_type x1, other arithmetic, per_device(): (inner_wide * inside_mask(tile_rows, tile_cols, 1)).astype(jnp.bfloat16)  1.84 us
  transfers between devices with their start and end apart: 4, of which 3 were waited for; matrix products, arithmetic and copies ran while one was open for 7% of the time, Pallas kernels for 0%

commit v1 on v0

v1 whole, which is shorter than its diff:
```python
import jax
import jax.numpy as jnp
from jax import lax
from jax.experimental import pallas as pl
from jax.experimental.pallas import tpu as pltpu
from jax.sharding import PartitionSpec as P

PADW = 112

def fused_kernel(flags, img, cot, top, bot, left, right, k1, k2, par, out, rowbuf, act3, cot3, in3):
    H, W, C = img.shape[1], img.shape[2], img.shape[3]
    half_one, bias_one = par[0:1, :], par[1:2, :]
    half_two, bias_two, scale_two_h = par[2:3, :], par[3:4, :], par[4:5, :]
    scale_one_h = par[5:6, :]

    def act_of(x):
        h = x.astype(jnp.float32) * half_one + bias_one
        return h * jnp.tanh(h) + h

    def fill(slot, h, own, lft, rgt, dst):
        rb = rowbuf.at[slot]
        rb[2 : 2 + W, :] = own
        rb[0:2, :] = lft
        rb[2 + W : 4 + W, :] = rgt
        for j in range(3):
            dst[j, h, :, :] = rb[j : j + PADW, :].astype(jnp.bfloat16)

    n = 0
    for h in range(H + 4):
        for which, dst in ((0, act3), (1, cot3)):
            if h < 2:
                own = top[which, h]
                m = flags[0]
            elif h >= H + 2:
                own = bot[which, h - H - 2]
                m = flags[1]
            else:
                own = (img if which == 0 else cot)[0, h - 2]
                m = None
            lft, rgt = left[which, h], right[which, h]
            if which == 0:
                own, lft, rgt = act_of(own), act_of(lft) * flags[2], act_of(rgt) * flags[3]
                if m is not None:
                    own, lft, rgt = own * m, lft * m, rgt * m
            else:
                own, lft, rgt = (v.astype(jnp.float32) for v in (own, lft, rgt))
            fill(n % 4, h, own, lft, rgt, dst)
            n += 1

    def conv(src, wref, base, rows, width, flip):
        acc = None
        for i in range(3):
            for j in range(3):
                lhs = src[j, base + i : base + i + rows, 0:width, :].reshape(rows * width, C)
                if flip:
                    t = lax.dot_general(lhs, wref[2 - i, 2 - j], (((1,), (1,)), ((), ())), preferred_element_type=jnp.float32)
                else:
                    t = lax.dot_general(lhs, wref[i, j], (((1,), (0,)), ((), ())), preferred_element_type=jnp.float32)
                acc = t if acc is None else acc + t
        return acc

    R = 6
    pos = lax.broadcasted_iota(jnp.int32, (PADW, 1), 0)
    cmask = jnp.where(pos == 0, flags[2], jnp.where(pos == W + 1, flags[3], 1.0))
    for b in range((H + 2) // R):
        c1 = conv(act3, k1, b * R, R, PADW, False)
        c2 = conv(cot3, k2, b * R, R, PADW, True)
        for r in range(R):
            h = b * R + r
            v = c1[r * PADW : (r + 1) * PADW] * half_two + bias_two
            t = jnp.tanh(v)
            s = (1.0 + t) * (1.0 + v - v * t)
            g = c2[r * PADW : (r + 1) * PADW] * scale_two_h * s * cmask
            if h == 0:
                g = g * flags[0]
            if h == H + 1:
                g = g * flags[1]
            rb = rowbuf.at[h % 4]
            rb[0:PADW, :] = g
            for j in range(3):
                in3[j, h, :, :] = rb[j : j + W, :].astype(jnp.bfloat16)
    R = 8
    for b in range(H // R):
        c3 = conv(in3, k1, b * R, R, W, True)
        for r in range(R):
            h = b * R + r
            v = img[0, h].astype(jnp.float32) * half_one + bias_one
            t = jnp.tanh(v)
            s = (1.0 + t) * (1.0 + v - v * t)
            res = cot[0, h].astype(jnp.float32) + c3[r * W : (r + 1) * W] * scale_one_h * s
            out[0, h] = res.astype(jnp.bfloat16)


def call(flags, img, cot, top, bot, left, right, k1, k2, par):
    H, W, C = img.shape[1:]
    vm = pl.BlockSpec(memory_space=pltpu.VMEM)
    return pl.pallas_call(
        fused_kernel,
        out_shape=jax.ShapeDtypeStruct(img.shape, jnp.bfloat16),
        in_specs=[pl.BlockSpec(memory_space=pltpu.SMEM)] + [vm] * 9,
        out_specs=vm,
        scratch_shapes=[
            pltpu.VMEM((4, PADW + 16, C), jnp.float32),
            pltpu.VMEM((3, H + 4, PADW, C), jnp.bfloat16),
            pltpu.VMEM((3, H + 4, PADW, C), jnp.bfloat16),
            pltpu.VMEM((3, H + 2, W, C), jnp.bfloat16),
        ],
        compiler_params=pltpu.CompilerParams(vmem_limit_bytes=48 << 20),
    )(flags, img, cot, top, bot, left, right, k1, k2, par)


def shifts(axis):
    size = lax.axis_size(axis)
    up = [(i, i + 1) for i in range(size - 1)]
    return up, [(j, i) for i, j in up]


def per_device(
    image_in,
    cotangent,
    first_kernel,
    first_bias,
    second_kernel,
    first_center,
    first_inverse,
    first_gain,
    first_shift,
    second_center,
    second_inverse,
    second_gain,
    second_shift,
):
    tile_cols = image_in.shape[2]
    repeats = image_in.shape[3] // first_center.shape[0]
    center_one = jnp.repeat(first_center, repeats)
    center_two = jnp.repeat(second_center, repeats)
    scale_one = jnp.repeat(first_inverse, repeats) * first_gain
    scale_two = jnp.repeat(second_inverse, repeats) * second_gain
    zero = jnp.zeros_like(scale_one)
    params = jnp.stack(
        (
            0.5 * scale_one,
            0.5 * (first_shift - center_one * scale_one),
            0.5 * scale_two,
            0.5 * ((first_bias - center_two) * scale_two + second_shift),
            0.5 * scale_two,
            0.5 * scale_one,
            zero,
            zero,
        )
    )
    row, col = lax.axis_index("rows"), lax.axis_index("cols")
    flags = jnp.stack(
        (row > 0, row < lax.axis_size("rows") - 1, col > 0, col < lax.axis_size("cols") - 1)
    ).astype(jnp.float32)
    pick = lambda *cut: jnp.concatenate((image_in[cut], cotangent[cut]))
    every = slice(None)
    up, down = shifts("rows")
    top = lax.ppermute(pick(every, slice(-2, None)), "rows", up)
    bottom = lax.ppermute(pick(every, slice(0, 2)), "rows", down)
    up, down = shifts("cols")
    edge = lambda cut: jnp.concatenate((top[:, :, cut], pick(every, every, cut), bottom[:, :, cut]), axis=1)
    left = lax.ppermute(edge(slice(tile_cols - 2, tile_cols)), "cols", up)
    right = lax.ppermute(edge(slice(0, 2)), "cols", down)
    return call(flags, image_in, cotangent, top, bottom, left, right, first_kernel, second_kernel, params)


def solution(mesh):
    tiled, whole = P(None, "rows", "cols", None), P()
    return jax.shard_map(
        per_device,
        mesh=mesh,
        in_specs=(tiled, tiled) + (whole,) * 11,
        out_specs=tiled,
        check_vma=False,
    )
```

time: 88.7 us -> 62.8 us (0.71)
  the two profiles are of different devices: /device:TPU:29 before, /device:TPU:27 now
where the time goes in v1:
time: 62.8 us; the launch traced here: 62.5 us
  starting transfers between devices  31.2 us (50%)
  waiting for transfers between devices  16.8 us (27%)
  Pallas kernels  9.48 us (15%)
  local copies, waits for them, and re-layouts  4.49 us (7%)
    ppermute x1, starting transfers between devices, per_device(): left = lax.ppermute(edge(slice(tile_cols - 2, tile_cols)), 'cols', up)  14.5 us
    ppermute x1, waiting for transfers between devices, per_device(): right = lax.ppermute(edge(slice(0, 2)), 'cols', down)  14.1 us
    ppermute x1, starting transfers between devices, per_device(): bottom = lax.ppermute(pick(every, slice(0, 2)), 'rows', down)  11.2 us
    pallas_call x1, Pallas kernels, call(): pl.pallas_call(fused_kernel, out_shape=jax.ShapeDtypeStruct(img.shape, jn...  9.48 us
    ppermute x1, starting transfers between devices, per_device(): top = lax.ppermute(pick(every, slice(-2, None)), 'rows', up)  3.55 us
    unnamed x26, local copies, waits for them, and re-layouts  2.59 us
    ppermute x1, starting transfers between devices, per_device(): right = lax.ppermute(edge(slice(0, 2)), 'cols', down)  1.92 us
    ppermute x1, waiting for transfers between devices, per_device(): top = lax.ppermute(pick(every, slice(-2, None)), 'rows', up)  1.76 us
  transfers between devices with their start and end apart: 4, of which 3 were waited for; matrix products, arithmetic and copies ran while one was open for 1% of the time, Pallas kernels for 0%

profile of v1, /device:TPU:27, one launch (start us, length us, event | category | flops | bytes accessed | tf_op | source)
XLA Modules:
  0.0 62.5 jit_solution(4845451198113855438)
XLA Ops:
  0.0 0.0 copy-start.1
  0.0 0.0 copy-start
  0.0 0.0 copy-start.9
  0.0 0.0 copy-start.10
  0.0 0.0 copy-start.11
  0.0 0.0 copy-start.12
  0.0 0.0 copy-start.4
  0.0 0.0 copy-start.6
  0.1 0.0 copy-start.5
  0.1 0.0 copy-start.7
  0.1 0.0 copy-start.8
  0.1 1.2 %fusion.2 = (bf16[1,2,96,256]{3,2,1,0:T(8,128)(2,1)S(1)}, bf16[1,2,96,256]{3,2,1,0:T(8,128)(2,1)S(1)}, bf16[1,2,96,256]{3,2,1,0:T(8,128)(2,1)S(1)}, bf16[1,2,96,256]{3,2,1,0:T(8,128)(2,1)S(1)}) fusion(bf16[1,16,96,256]{3,2,1,0:T(8,128)(2,1)} %img.1, bf16[1,16,96,256]{3,2,1,0:T(8,128)(2,1)} %cot.1), kind=kLoop, calls=%fused_computation.11 | loop fusion | bytes 786432 | tf_op jit(solution)/shard_map/slice | solution.py:156
  1.3 3.5 %collective-permute-start = (bf16[2,2,96,256]{3,2,1,0:T(8,128)(2,1)S(1)}, bf16[2,2,96,256]{3,2,1,0:T(8,128)(2,1)S(1)}, u32[]{:S(2)}, u32[]{:S(2)}) collective-permute-start(bf16[2,2,96,256]{3,2,1,0:T(8,128)(2,1)S(1)} %pad_maximum_fusion), channel_id=1, source_target_pairs={{0,16},{16,32},{32,48},{48,64},{64,80},{80,96},{96,112},{112,128},... | collective-permute-start | bytes 589832 | tf_op jit(solution)/shard_map/ppermute | solution.py:159
  4.9 11.2 %collective-permute-start.1 = (bf16[2,2,96,256]{3,2,1,0:T(8,128)(2,1)S(1)}, bf16[2,2,96,256]{3,2,1,0:T(8,128)(2,1)S(1)}, u32[]{:S(2)}, u32[]{:S(2)}) collective-permute-start(bf16[2,2,96,256]{3,2,1,0:T(8,128)(2,1)S(1)} %pad_maximum_fusion.1), channel_id=1, source_target_pairs={{16,0},{32,16},{48,32},{64,48},{80,64},{96,80},{112,96},{128,112},... | collective-permute-start | bytes 589832 | tf_op jit(solution)/shard_map/ppermute | solution.py:160
  16.1 0.0 copy-done.1
  16.1 0.0 copy-done
  16.1 0.1 fusion
  16.2 0.0 copy-done.9
  16.2 0.1 broadcast_in_dim.13
  16.3 0.1 reshape.13
  16.4 0.0 copy-done.10
  16.4 0.1 broadcast_in_dim.12
  16.5 0.1 reshape.12
  16.5 0.0 copy-done.11
  16.6 0.1 broadcast_in_dim.15
  16.6 0.1 reshape.15
  16.7 0.0 copy-done.12
  16.7 0.1 broadcast_in_dim.14
  16.8 0.1 reshape.14
  16.9 0.0 copy-done.4
  16.9 0.0 copy-done.6
  16.9 0.0 copy-done.5
  16.9 0.0 copy-done.7
  16.9 0.0 copy-done.8
  17.0 1.8 %collective-permute-done.top = bf16[2,2,96,256]{3,2,1,0:T(8,128)(2,1)S(1)} collective-permute-done((bf16[2,2,96,256]{3,2,1,0:T(8,128)(2,1)S(1)}, bf16[2,2,96,256]{3,2,1,0:T(8,128)(2,1)S(1)}, u32[]{:S(2)}, u32[]{:S(2)}) %collective-permute-start) | collective-permute-done | bytes 196640 | tf_op jit(solution)/shard_map/ppermute | solution.py:159
  18.7 0.9 %collective-permute-done.1.bot = bf16[2,2,96,256]{3,2,1,0:T(8,128)(2,1)S(1)} collective-permute-done((bf16[2,2,96,256]{3,2,1,0:T(8,128)(2,1)S(1)}, bf16[2,2,96,256]{3,2,1,0:T(8,128)(2,1)S(1)}, u32[]{:S(2)}, u32[]{:S(2)}) %collective-permute-start.1) | collective-permute-done | bytes 196640 | tf_op jit(solution)/shard_map/ppermute | solution.py:160
  19.7 0.1 pad_maximum_fusion.2
  19.8 14.5 %collective-permute-start.2 = (bf16[2,20,2,256]{3,2,1,0:T(2,128)(2,1)S(1)}, bf16[2,20,2,256]{3,2,1,0:T(2,128)(2,1)S(1)}, u32[]{:S(2)}, u32[]{:S(2)}) collective-permute-start(bf16[2,20,2,256]{3,2,1,0:T(2,128)(2,1)S(1)} %pad_maximum_fusion.2), channel_id=1, source_target_pairs={{0,1},{1,2},{2,3},{3,4},{4,5},{5,6},{6,7},{7,8},{8,9},{9,10},{10,1... | collective-permute-start | bytes 122888 | tf_op jit(solution)/shard_map/ppermute | solution.py:163
  34.3 0.1 pad_maximum_fusion.3
  34.4 1.9 %collective-permute-start.3 = (bf16[2,20,2,256]{3,2,1,0:T(2,128)(2,1)S(1)}, bf16[2,20,2,256]{3,2,1,0:T(2,128)(2,1)S(1)}, u32[]{:S(2)}, u32[]{:S(2)}) collective-permute-start(bf16[2,20,2,256]{3,2,1,0:T(2,128)(2,1)S(1)} %pad_maximum_fusion.3), channel_id=1, source_target_pairs={{1,0},{2,1},{3,2},{4,3},{5,4},{6,5},{7,6},{8,7},{9,8},{10,9},{11,1... | collective-permute-start | bytes 122888 | tf_op jit(solution)/shard_map/ppermute | solution.py:164
  36.3 0.1 add_convert_fusion.flags
  36.4 0.0 collective-permute-done.2.left
  36.4 14.1 %collective-permute-done.3.right = bf16[2,20,2,256]{3,2,1,0:T(2,128)(2,1)S(1)} collective-permute-done((bf16[2,20,2,256]{3,2,1,0:T(2,128)(2,1)S(1)}, bf16[2,20,2,256]{3,2,1,0:T(2,128)(2,1)S(1)}, u32[]{:S(2)}, u32[]{:S(2)}) %collective-permute-start.3) | collective-permute-done | bytes 40992 | tf_op jit(solution)/shard_map/ppermute | solution.py:164
  50.5 0.0 copy-start.2
  50.5 1.3 %copy-done.2 = bf16[3,3,256,256]{3,2,1,0:T(8,128)(2,1)S(1)} copy-done((bf16[3,3,256,256]{3,2,1,0:T(8,128)(2,1)S(1)}, bf16[3,3,256,256]{3,2,1,0:T(8,128)(2,1)}, u32[]{:S(2)}) %copy-start.2) | copy-done | bytes 1179672
  51.8 0.0 copy-start.3
  51.8 1.3 %copy-done.3 = bf16[3,3,256,256]{3,2,1,0:T(8,128)(2,1)S(1)} copy-done((bf16[3,3,256,256]{3,2,1,0:T(8,128)(2,1)S(1)}, bf16[3,3,256,256]{3,2,1,0:T(8,128)(2,1)}, u32[]{:S(2)}) %copy-start.3) | copy-done | bytes 1179672
  53.1 9.5 %shard_map.127 = bf16[1,16,96,256]{3,2,1,0:T(8,128)(2,1)} custom-call(f32[4]{0:T(128)S(1)} %add_convert_fusion.flags, bf16[1,16,96,256]{3,2,1,0:T(8,128)(2,1)S(1)} %copy-done, bf16[1,16,96,256]{3,2,1,0:T(8,128)(2,1)S(1)} %copy-done.1, bf16[2,2,96,256]{3,2,1,0:T(8,128)(2,1)S(1)} %collective-permute-done.top, ...), custom_call_target="tpu_custom_call" | custom-call | tf_op jit(solution)/shard_map/pallas_call | solution.py:97
  (8 shorter events, 0.1 us)
Async XLA Ops:
  0.0 16.1 %copy-start.1 = (bf16[1,16,96,256]{3,2,1,0:T(8,128)(2,1)S(1)}, bf16[1,16,96,256]{3,2,1,0:T(8,128)(2,1)}, u32[]{:S(2)}) copy-start(bf16[1,16,96,256]{3,2,1,0:T(8,128)(2,1)} %cot.1) | copy-start | bytes 2359300
  0.0 16.1 %copy-start = (bf16[1,16,96,256]{3,2,1,0:T(8,128)(2,1)S(1)}, bf16[1,16,96,256]{3,2,1,0:T(8,128)(2,1)}, u32[]{:S(2)}) copy-start(bf16[1,16,96,256]{3,2,1,0:T(8,128)(2,1)} %img.1) | copy-start | bytes 2359300
  0.0 16.2 %copy-start.9 = (f32[32]{0:T(128)S(1)}, f32[32]{0:T(128)}, u32[]{:S(2)}) copy-start(f32[32]{0:T(128)} %param.18) | copy-start | bytes 388
  0.0 16.4 %copy-start.10 = (f32[32]{0:T(128)S(1)}, f32[32]{0:T(128)}, u32[]{:S(2)}) copy-start(f32[32]{0:T(128)} %param.19) | copy-start | bytes 388
  0.0 16.5 %copy-start.11 = (f32[32]{0:T(128)S(1)}, f32[32]{0:T(128)}, u32[]{:S(2)}) copy-start(f32[32]{0:T(128)} %param.22) | copy-start | bytes 388
  0.0 16.7 %copy-start.12 = (f32[32]{0:T(128)S(1)}, f32[32]{0:T(128)}, u32[]{:S(2)}) copy-start(f32[32]{0:T(128)} %param.23) | copy-start | bytes 388
  0.0 16.9 %copy-start.4 = (f32[256]{0:T(256)S(1)}, f32[256]{0:T(256)}, u32[]{:S(2)}) copy-start(f32[256]{0:T(256)} %param.25) | copy-start | bytes 3076
  0.0 16.9 %copy-start.6 = (f32[256]{0:T(256)S(1)}, f32[256]{0:T(256)}, u32[]{:S(2)}) copy-start(f32[256]{0:T(256)} %param.24) | copy-start | bytes 3076
  0.1 16.9 %copy-start.5 = (f32[256]{0:T(256)S(1)}, f32[256]{0:T(256)}, u32[]{:S(2)}) copy-start(f32[256]{0:T(256)} %param.16) | copy-start | bytes 3076
  0.1 16.9 %copy-start.7 = (f32[256]{0:T(256)S(1)}, f32[256]{0:T(256)}, u32[]{:S(2)}) copy-start(f32[256]{0:T(256)} %param.21) | copy-start | bytes 3076
  0.1 16.9 %copy-start.8 = (f32[256]{0:T(256)S(1)}, f32[256]{0:T(256)}, u32[]{:S(2)}) copy-start(f32[256]{0:T(256)} %param.20) | copy-start | bytes 3076
  1.3 17.4 %collective-permute-start = (bf16[2,2,96,256]{3,2,1,0:T(8,128)(2,1)S(1)}, bf16[2,2,96,256]{3,2,1,0:T(8,128)(2,1)S(1)}, u32[]{:S(2)}, u32[]{:S(2)}) collective-permute-start(bf16[2,2,96,256]{3,2,1,0:T(8,128)(2,1)S(1)} %pad_maximum_fusion), channel_id=1, source_target_pairs={{0,16},{16,32},{32,48},{48,64},{64,80},{80,96},{96,112},{112,128},... | collective-permute-start | bytes 589832 | tf_op jit(solution)/shard_map/ppermute | solution.py:159
  4.9 14.8 %collective-permute-start.1 = (bf16[2,2,96,256]{3,2,1,0:T(8,128)(2,1)S(1)}, bf16[2,2,96,256]{3,2,1,0:T(8,128)(2,1)S(1)}, u32[]{:S(2)}, u32[]{:S(2)}) collective-permute-start(bf16[2,2,96,256]{3,2,1,0:T(8,128)(2,1)S(1)} %pad_maximum_fusion.1), channel_id=1, source_target_pairs={{16,0},{32,16},{48,32},{64,48},{80,64},{96,80},{112,96},{128,112},... | collective-permute-start | bytes 589832 | tf_op jit(solution)/shard_map/ppermute | solution.py:160
  19.8 16.7 %collective-permute-start.2 = (bf16[2,20,2,256]{3,2,1,0:T(2,128)(2,1)S(1)}, bf16[2,20,2,256]{3,2,1,0:T(2,128)(2,1)S(1)}, u32[]{:S(2)}, u32[]{:S(2)}) collective-permute-start(bf16[2,20,2,256]{3,2,1,0:T(2,128)(2,1)S(1)} %pad_maximum_fusion.2), channel_id=1, source_target_pairs={{0,1},{1,2},{2,3},{3,4},{4,5},{5,6},{6,7},{7,8},{8,9},{9,10},{10,1... | collective-permute-start | bytes 122888 | tf_op jit(solution)/shard_map/ppermute | solution.py:163
  34.4 16.1 %collective-permute-start.3 = (bf16[2,20,2,256]{3,2,1,0:T(2,128)(2,1)S(1)}, bf16[2,20,2,256]{3,2,1,0:T(2,128)(2,1)S(1)}, u32[]{:S(2)}, u32[]{:S(2)}) collective-permute-start(bf16[2,20,2,256]{3,2,1,0:T(2,128)(2,1)S(1)} %pad_maximum_fusion.3), channel_id=1, source_target_pairs={{1,0},{2,1},{3,2},{4,3},{5,4},{6,5},{7,6},{8,7},{9,8},{10,9},{11,1... | collective-permute-start | bytes 122888 | tf_op jit(solution)/shard_map/ppermute | solution.py:164
  50.5 1.3 %copy-start.2 = (bf16[3,3,256,256]{3,2,1,0:T(8,128)(2,1)S(1)}, bf16[3,3,256,256]{3,2,1,0:T(8,128)(2,1)}, u32[]{:S(2)}) copy-start(bf16[3,3,256,256]{3,2,1,0:T(8,128)(2,1)} %k1.1) | copy-start | bytes 3538948
  51.8 1.3 %copy-start.3 = (bf16[3,3,256,256]{3,2,1,0:T(8,128)(2,1)S(1)}, bf16[3,3,256,256]{3,2,1,0:T(8,128)(2,1)}, u32[]{:S(2)}) copy-start(bf16[3,3,256,256]{3,2,1,0:T(8,128)(2,1)} %k2.1) | copy-start | bytes 3538948

commit v2 on v0

v2 whole, which is shorter than its diff:
```python
import jax
import jax.numpy as jnp
from jax import lax
from jax.experimental import pallas as pl
from jax.experimental.pallas import tpu as pltpu
from jax.sharding import PartitionSpec as P

PADW = 112
F32, BF16 = jnp.float32, jnp.bfloat16
ROWS, COLS = "rows", "cols"
VMEM, HBM, SMEM = (pl.BlockSpec(memory_space=m) for m in (pltpu.VMEM, pltpu.HBM, pltpu.SMEM))
LIMIT = pltpu.CompilerParams(vmem_limit_bytes=40 << 20)


def place():
    row, col = lax.axis_index(ROWS), lax.axis_index(COLS)
    rows, cols = lax.axis_size(ROWS), lax.axis_size(COLS)
    exists = [x.astype(jnp.int32).astype(F32) for x in (row > 0, row < rows - 1, col > 0, col < cols - 1)]
    return row % 2 == 1, col % 2 == 1, exists


def edges_kernel(img, cot, near, far, lo, hi, strip, sems):
    H, W, _ = img.shape[1:]
    copies = []
    for k, x in enumerate((img, cot)):
        copies += [
            pltpu.make_async_copy(x.at[0, :, 0:8, :], lo.at[k], sems.at[2 * k]),
            pltpu.make_async_copy(x.at[0, :, W - 8 : W, :], hi.at[k], sems.at[2 * k + 1]),
        ]
    for c in copies:
        c.start()
    _, odd_col, _ = place()
    for k in range(2):
        copies[2 * k].wait()
        copies[2 * k + 1].wait()
        for h in range(H):
            strip[0, 2 * h : 2 * h + 2, :] = lo[k, h].astype(F32)[0:2]
            strip[1, 2 * h : 2 * h + 2, :] = hi[k, h].astype(F32)[6:8]
        first, last = strip[0].astype(BF16), strip[1].astype(BF16)
        near[k] = jnp.where(odd_col, first, last)
        far[k] = jnp.where(odd_col, last, first)


def edges(img, cot):
    H, _, C = img.shape[1:]
    shape = jax.ShapeDtypeStruct((2, 2 * H, C), BF16)
    return pl.pallas_call(
        edges_kernel,
        out_shape=(shape, shape),
        in_specs=[HBM, HBM],
        out_specs=(VMEM, VMEM),
        scratch_shapes=[
            pltpu.VMEM((2, H, 8, C), BF16),
            pltpu.VMEM((2, H, 8, C), BF16),
            pltpu.VMEM((2, 2 * H, C), F32),
            pltpu.SemaphoreType.DMA((4,)),
        ],
        name="edges",
    )(img, cot)


def messages_kernel(img, cot, ce, co, odd, even, near_own, far_own, buf):
    H, W = img.shape[1], img.shape[2]
    n, m = 2 * W, ce.shape[1]
    odd_row, _, _ = place()
    buf[8:16] = jnp.zeros_like(buf[8:16])
    for k in range(2):
        near_own[k], far_own[k] = ce[k], co[k]
        x = (img, cot)[k]
        for h in range(2):
            upper, lower = x[0, h], x[0, H - 2 + h]
            odd[k, h * W : (h + 1) * W] = jnp.where(odd_row, lower, upper)
            even[k, h * W : (h + 1) * W] = jnp.where(odd_row, upper, lower)
        tops = [r[k, 0:16].astype(F32)[0:4] for r in (ce, co)]
        ends = [r[k, m - 16 : m].astype(F32)[12:16] for r in (ce, co)]
        for dst, flip in ((odd, False), (even, True)):
            for s in range(2):
                first, second = (tops[s], ends[s]) if flip else (ends[s], tops[s])
                buf[4 * s : 4 * s + 4] = jnp.where(odd_row, first, second)
            dst[k, n : n + 16] = buf[...].astype(BF16)


def messages(img, cot, ce, co):
    n, m, C = 2 * img.shape[2], ce.shape[1], ce.shape[2]
    shape = lambda n: jax.ShapeDtypeStruct((2, n, C), BF16)
    return pl.pallas_call(
        messages_kernel,
        out_shape=(shape(n + 16), shape(n + 16), shape(m), shape(m)),
        in_specs=[VMEM] * 4,
        out_specs=(VMEM,) * 4,
        scratch_shapes=[pltpu.VMEM((16, C), F32)],
        name="messages",
    )(img, cot, ce, co)


def per_channel(stat, channels):
    group = lax.broadcasted_iota(jnp.int32, (1, channels), 1) // (channels // stat.shape[0])
    wide = jnp.full((1, channels), stat[0], F32)
    for g in range(1, stat.shape[0]):
        wide = jnp.where(group == g, stat[g], wide)
    return wide


def affine(stats, vecs, C):
    center_one, inverse_one, center_two, inverse_two = (per_channel(v, C) for v in stats)
    bias, gain_one, shift_one, gain_two, shift_two = (v[0:1, :] for v in vecs)
    half_one, half_two = 0.5 * (inverse_one * gain_one), 0.5 * (inverse_two * gain_two)
    bias_one = 0.5 * shift_one - center_one * half_one
    bias_two = (bias - center_two) * half_two + 0.5 * shift_two
    return half_one, bias_one, half_two, bias_two


def act_of(x, half, bias):
    h = x.astype(F32) * half + bias
    return h * jnp.tanh(h) + h


def slope_of(v):
    t = jnp.tanh(v)
    return (1.0 + t) * (1.0 + v - v * t)


def fill(rb, own, lft, rgt, dst, h):
    W = own.shape[0]
    rb[2 : 2 + W, :] = own.astype(F32)
    rb[0:2, :] = lft
    rb[2 + W : 4 + W, :] = rgt
    for j in range(3):
        dst[j, h, :, :] = rb[j : j + PADW, :].astype(BF16)


def conv(src, wref, starts, rows, width, flip):
    C, acc = wref.shape[3], None
    for i in range(3):
        for j in range(3):
            parts = [src[j, b + i : b + i + rows, 0:width, :].reshape(rows * width, C) for b in starts]
            lhs = parts[0] if len(parts) == 1 else jnp.concatenate(parts)
            w = wref[2 - i, 2 - j] if flip else wref[i, j]
            dims = (((1,), (1 if flip else 0,)), ((), ()))
            t = lax.dot_general(lhs, w, dims, preferred_element_type=F32)
            acc = t if acc is None else acc + t
    return acc


def inner_rows(c1, c2, r, half_two, bias_two, cmask):
    cut = slice(r * PADW, (r + 1) * PADW)
    return c2[cut] * half_two * slope_of(c1[cut] * half_two + bias_two) * cmask


def store_inner(rb, g, dst, h, W):
    rb[0:PADW, :] = g
    for j in range(3):
        dst[j, h, :, :] = rb[j : j + W, :].astype(BF16)


def col_mask(to_left, to_right, W):
    pos = lax.broadcasted_iota(jnp.int32, (PADW, 1), 0)
    return jnp.where(pos == 0, to_left, jnp.where(pos == W + 1, to_right, 1.0))


def result_row(x, g, c3, half_one, bias_one):
    v = x.astype(F32) * half_one + bias_one
    return (g.astype(F32) + c3 * half_one * slope_of(v)).astype(BF16)


def middle_kernel(
    stats, vecs, img, cot, ce, co, w1, w2, out, kept, rowbuf, act3, cot3, in3, res, nbuf, fbuf, k1, k2, sems
):
    H, W, C = img.shape[1:]
    loads = [pltpu.make_async_copy(w1, k1, sems.at[0]), pltpu.make_async_copy(w2, k2, sems.at[1])]
    for load in loads:
        load.start()
    half_one, bias_one, half_two, bias_two = affine(stats, vecs, C)
    odd_row, odd_col, (up, down, to_left, to_right) = place()
    for k in range(2):
        nbuf[k], fbuf[k] = ce[k].astype(F32), co[k].astype(F32)
    count = 0
    for h in range(H):
        for k, (src, dst) in enumerate(((img, act3), (cot, cot3))):
            cut = slice(2 * h, 2 * h + 2)
            near, far = nbuf[k, cut], fbuf[k, cut]
            lft, rgt = jnp.where(odd_col, near, far), jnp.where(odd_col, far, near)
            own = src[0, h]
            if k == 0:
                own = act_of(own, half_one, bias_one)
                lft, rgt = act_of(lft, half_one, bias_one) * to_left, act_of(rgt, half_one, bias_one) * to_right
            fill(rowbuf.at[count % 4], own, lft, rgt, dst, h)
            count += 1
    for load in loads:
        load.wait()
    cmask = col_mask(to_left, to_right, W)
    R = (H - 2) // 2
    for b in range(0, H - 2, R):
        c1 = conv(act3, k1, (b,), R, PADW, False)
        c2 = conv(cot3, k2, (b,), R, PADW, True)
        for r in range(R):
            g = inner_rows(c1, c2, r, half_two, bias_two, cmask)
            store_inner(rowbuf.at[r % 4], g, in3, b + r, W)
    for j in range(3):
        for s, h in enumerate((0, 1, H - 4, H - 3)):
            kept[j, s] = in3[j, h]
    R = (H - 4) // 2
    stores = []
    for b in range(0, H - 4, R):
        c3 = conv(in3, k1, (b,), R, W, True)
        for r in range(R):
            h = b + r + 2
            res[b + r] = result_row(img[0, h], cot[0, h], c3[r * W : (r + 1) * W], half_one, bias_one)
        stores.append(pltpu.make_async_copy(res.at[b : b + R], out.at[0, b + 2 : b + 2 + R], sems.at[2 + b // R]))
        stores[-1].start()
    for store in stores:
        store.wait()


def middle(stats, vecs, img, cot, ce, co, k1, k2):
    H, W, C = img.shape[1:]
    return pl.pallas_call(
        middle_kernel,
        out_shape=(jax.ShapeDtypeStruct(img.shape, BF16), jax.ShapeDtypeStruct((3, 4, W, C), BF16)),
        in_specs=[(SMEM,) * 4, (VMEM,) * 5] + [VMEM] * 4 + [HBM, HBM],
        out_specs=(HBM, VMEM),
        scratch_shapes=[
            pltpu.VMEM((4, PADW + 16, C), F32),
            pltpu.VMEM((3, H, PADW, C), BF16),
            pltpu.VMEM((3, H, PADW, C), BF16),
            pltpu.VMEM((3, H - 2, W, C), BF16),
            pltpu.VMEM((H - 4, W, C), BF16),
            pltpu.VMEM((2, 2 * H, C), F32),
            pltpu.VMEM((2, 2 * H, C), F32),
            pltpu.VMEM(k1.shape, BF16),
            pltpu.VMEM(k2.shape, BF16),
            pltpu.SemaphoreType.DMA((4,)),
        ],
        compiler_params=LIMIT,
        name="middle",
    )(stats, vecs, img, cot, ce, co, k1, k2)


def border_kernel(
    stats, vecs, img, cot, ce, co, odd, even, w1, w2, kept, old, out,
    rowbuf, act3, cot3, in3, res, nbuf, fbuf, k1, k2, sems,
):
    H, W, C = img.shape[1:]
    m = 2 * H
    loads = [pltpu.make_async_copy(w1, k1, sems.at[0]), pltpu.make_async_copy(w2, k2, sems.at[1])]
    for load in loads:
        load.start()
    half_one, bias_one, half_two, bias_two = affine(stats, vecs, C)
    odd_row, odd_col, (up, down, to_left, to_right) = place()
    for k in range(2):
        nbuf[k, 4 : m + 4], fbuf[k, 4 : m + 4] = ce[k].astype(F32), co[k].astype(F32)
        o, e = odd[k, 2 * W : 2 * W + 16].astype(F32), even[k, 2 * W : 2 * W + 16].astype(F32)
        near_odd, near_even, far_odd, far_even = o[0:4], e[0:4], o[4:8], e[4:8]
        nbuf[k, 0:4] = jnp.where(odd_row, near_even, near_odd)
        nbuf[k, m + 4 : m + 8] = jnp.where(odd_row, near_odd, near_even)
        fbuf[k, 0:4] = jnp.where(odd_row, far_even, far_odd)
        fbuf[k, m + 4 : m + 8] = jnp.where(odd_row, far_odd, far_even)
    count = 0
    for s, h in enumerate((0, 1, 2, 3, H, H + 1, H + 2, H + 3)):
        for k, (src, dst) in enumerate(((img, act3), (cot, cot3))):
            mask = None
            if h < 2 or h >= H + 2:
                t = h if h < 2 else h - H - 2
                cut = slice(t * W, (t + 1) * W)
                o, e = odd[k, cut], even[k, cut]
                own = jnp.where(odd_row, e, o) if h < 2 else jnp.where(odd_row, o, e)
                mask = up if h < 2 else down
            else:
                own = src[0, h - 2]
            near, far = nbuf[k, 2 * h : 2 * h + 2], fbuf[k, 2 * h : 2 * h + 2]
            lft, rgt = jnp.where(odd_col, near, far), jnp.where(odd_col, far, near)
            if k == 0:
                own = act_of(own, half_one, bias_one)
                lft, rgt = act_of(lft, half_one, bias_one) * to_left, act_of(rgt, half_one, bias_one) * to_right
                if mask is not None:
                    own, lft, rgt = own * mask, lft * mask, rgt * mask
            fill(rowbuf.at[count % 4], own, lft, rgt, dst, s)
            count += 1
    for j in range(3):
        for s, d in enumerate((2, 3, 4, 5)):
            in3[j, d] = kept[j, s]
    for load in loads:
        load.wait()
    cmask = col_mask(to_left, to_right, W)
    c1 = conv(act3, k1, (0, 4), 2, PADW, False)
    c2 = conv(cot3, k2, (0, 4), 2, PADW, True)
    for r, (d, mask) in enumerate(((0, up), (1, None), (6, None), (7, down))):
        g = inner_rows(c1, c2, r, half_two, bias_two, cmask)
        store_inner(rowbuf.at[r], g if mask is None else g * mask, in3, d, W)
    c3 = conv(in3, k1, (0, 4), 2, W, True)
    for r, h in enumerate((0, 1, H - 2, H - 1)):
        res[r] = result_row(img[0, h], cot[0, h], c3[r * W : (r + 1) * W], half_one, bias_one)
    stores = [
        pltpu.make_async_copy(res.at[0:2], out.at[0, 0:2], sems.at[2]),
        pltpu.make_async_copy(res.at[2:4], out.at[0, H - 2 : H], sems.at[3]),
    ]
    for store in stores:
        store.start()
    for store in stores:
        store.wait()


def border(stats, vecs, img, cot, ce, co, odd, even, k1, k2, kept, old):
    H, W, C = img.shape[1:]
    return pl.pallas_call(
        border_kernel,
        out_shape=jax.ShapeDtypeStruct(img.shape, BF16),
        in_specs=[(SMEM,) * 4, (VMEM,) * 5] + [VMEM] * 6 + [HBM, HBM, VMEM, HBM],
        out_specs=HBM,
        input_output_aliases={4 + 5 + 6 + 3: 0},
        scratch_shapes=[
            pltpu.VMEM((4, PADW + 16, C), F32),
            pltpu.VMEM((3, 8, PADW, C), BF16),
            pltpu.VMEM((3, 8, PADW, C), BF16),
            pltpu.VMEM((3, 8, W, C), BF16),
            pltpu.VMEM((4, W, C), BF16),
            pltpu.VMEM((2, 2 * H + 8, C), F32),
            pltpu.VMEM((2, 2 * H + 8, C), F32),
            pltpu.VMEM(k1.shape, BF16),
            pltpu.VMEM(k2.shape, BF16),
            pltpu.SemaphoreType.DMA((4,)),
        ],
        compiler_params=LIMIT,
        name="border",
    )(stats, vecs, img, cot, ce, co, odd, even, k1, k2, kept, old)


def swaps(size, first):
    return [pair for i in range(first, size - 1, 2) for pair in ((i, i + 1), (i + 1, i))]


def per_device(
    image_in,
    cotangent,
    first_kernel,
    first_bias,
    second_kernel,
    first_center,
    first_inverse,
    first_gain,
    first_shift,
    second_center,
    second_inverse,
    second_gain,
    second_shift,
):
    stats = (first_center, first_inverse, second_center, second_inverse)
    vecs = tuple(v[None] for v in (first_bias, first_gain, first_shift, second_gain, second_shift))
    def send(name, x):
        axis = COLS if name[0] == "c" else ROWS
        return lax.ppermute(x, axis, swaps(lax.axis_size(axis), int(name[1] == "o")))

    stay = lambda x: pltpu.with_memory_space_constraint(x, pltpu.HBM)
    first_kernel, second_kernel = stay(first_kernel), stay(second_kernel)
    near, far = edges(image_in, cotangent)
    co, ce = send("co", far), send("ce", near)
    odd, even, ce, co = messages(image_in, cotangent, ce, co)
    odd, even = send("ro", odd), send("re", even)
    out, kept = middle(stats, vecs, image_in, cotangent, ce, co, first_kernel, second_kernel)
    return border(stats, vecs, image_in, cotangent, ce, co, odd, even, first_kernel, second_kernel, kept, out)


def solution(mesh):
    tiled, whole = P(None, ROWS, COLS, None), P()
    return jax.shard_map(
        per_device,
        mesh=mesh,
        in_specs=(tiled, tiled) + (whole,) * 11,
        out_specs=tiled,
        check_vma=False,
    )
```

time: 88.7 us -> 54.9 us (0.62)
  the two profiles are of different devices: /device:TPU:29 before, /device:TPU:31 now
where the time goes in v2:
time: 54.9 us; the launch traced here: 54.4 us
  starting transfers between devices  32.3 us (59%)
  Pallas kernels  17.9 us (33%)
  local copies, waits for them, and re-layouts  2.18 us (4%)
  waiting for transfers between devices  1.78 us (3%)
    ppermute x4, starting transfers between devices, send(): lax.ppermute(x, axis, swaps(lax.axis_size(axis), int(name[1] == 'o')))  32.3 us
    pallas_call x1, Pallas kernels, middle(): pl.pallas_call(middle_kernel, out_shape=(jax.ShapeDtypeStruct(img.shape,...  8.66 us
    pallas_call x1, Pallas kernels, border(): pl.pallas_call(border_kernel, out_shape=jax.ShapeDtypeStruct(img.shape, B...  5.38 us
    pallas_call x1, Pallas kernels, messages(): pl.pallas_call(messages_kernel, out_shape=(shape(n + 16), shape(n + 16),...  2.21 us
    unnamed x30, local copies, waits for them, and re-layouts  2.18 us
    ppermute x4, waiting for transfers between devices, send(): lax.ppermute(x, axis, swaps(lax.axis_size(axis), int(name[1] == 'o')))  1.78 us
    pallas_call x1, Pallas kernels, edges(): pl.pallas_call(edges_kernel, out_shape=(shape, shape), in_specs=[HBM, HBM...  1.62 us
  transfers between devices with their start and end apart: 4, of which 1 were waited for; matrix products, arithmetic and copies ran while one was open for 0% of the time, Pallas kernels for 16%

profile of v2, /device:TPU:31, one launch (start us, length us, event | category | flops | bytes accessed | tf_op | source)
XLA Modules:
  0.0 54.4 jit_solution(4114527617897938443)
XLA Ops:
  0.0 1.6 %edges.1 = (bf16[2,32,256]{2,1,0:T(8,128)(2,1)}, bf16[2,32,256]{2,1,0:T(8,128)(2,1)}) custom-call(bf16[1,16,96,256]{3,2,1,0:T(8,128)(2,1)} %img.7, bf16[1,16,96,256]{3,2,1,0:T(8,128)(2,1)} %cot.7), custom_call_target="tpu_custom_call" | custom-call | tf_op jit(solution)/shard_map/edges/pallas_call | solution.py:47
  1.6 0.0 copy-start
  1.6 0.0 copy-start.1
  1.6 0.0 copy-start.4
  1.7 0.0 copy-start.5
  1.7 0.0 copy-start.6
  1.7 0.0 copy-start.7
  1.7 0.0 copy-start.8
  1.7 0.0 copy-start.9
  1.7 0.0 copy-start.10
  1.7 0.0 copy-start.11
  1.7 0.0 copy-start.12
  1.8 2.7 %collective-permute-start = (bf16[2,32,256]{2,1,0:T(8,128)(2,1)}, bf16[2,32,256]{2,1,0:T(8,128)(2,1)S(1)}, u32[]{:S(2)}, u32[]{:S(2)}) collective-permute-start(bf16[2,32,256]{2,1,0:T(8,128)(2,1)} %get-tuple-element.13), channel_id=1, source_target_pairs={{0,1},{1,0},{2,3},{3,2},{4,5},{5,4},{6,7},{7,6},{8,9},{9,8},{10,11... | collective-permute-start | bytes 98312 | tf_op jit(solution)/shard_map/ppermute | solution.py:351
  4.5 15.0 %collective-permute-start.1 = (bf16[2,32,256]{2,1,0:T(8,128)(2,1)}, bf16[2,32,256]{2,1,0:T(8,128)(2,1)S(1)}, u32[]{:S(2)}, u32[]{:S(2)}) collective-permute-start(bf16[2,32,256]{2,1,0:T(8,128)(2,1)} %get-tuple-element.14), channel_id=1, source_target_pairs={{1,2},{2,1},{3,4},{4,3},{5,6},{6,5},{7,8},{8,7},{9,10},{10,9},{11,... | collective-permute-start | bytes 98312 | tf_op jit(solution)/shard_map/ppermute | solution.py:351
  19.5 0.0 collective-permute-done.ce
  19.5 0.0 copy-start.13
  19.5 1.8 %collective-permute-done.1.co = bf16[2,32,256]{2,1,0:T(8,128)(2,1)S(1)} collective-permute-done((bf16[2,32,256]{2,1,0:T(8,128)(2,1)}, bf16[2,32,256]{2,1,0:T(8,128)(2,1)S(1)}, u32[]{:S(2)}, u32[]{:S(2)}) %collective-permute-start.1) | collective-permute-done | bytes 32800 | tf_op jit(solution)/shard_map/ppermute | solution.py:351
  21.3 0.0 copy-done.13
  21.3 0.0 copy-start.14
  21.3 0.6 %copy-done.14 = bf16[2,32,256]{2,1,0:T(8,128)(2,1)} copy-done((bf16[2,32,256]{2,1,0:T(8,128)(2,1)}, bf16[2,32,256]{2,1,0:T(8,128)(2,1)S(1)}, u32[]{:S(2)}) %copy-start.14) | copy-done | bytes 32792
  21.9 2.2 %messages.1 = (bf16[2,208,256]{2,1,0:T(8,128)(2,1)}, bf16[2,208,256]{2,1,0:T(8,128)(2,1)}, bf16[2,32,256]{2,1,0:T(8,128)(2,1)}, bf16[2,32,256]{2,1,0:T(8,128)(2,1)}) custom-call(bf16[1,16,96,256]{3,2,1,0:T(8,128)(2,1)} %img.7, bf16[1,16,96,256]{3,2,1,0:T(8,128)(2,1)} %cot.7, bf16[2,32,256]{2,1,0:T(8,128)(2,1)} %copy-done.13, bf16[2,32,256]{2,1,0:T(8,128)(2,1)} %copy-done.14), custom_call_target="tpu_custom_call" | custom-call | tf_op jit(solution)/shard_map/messages/pallas_call | solution.py:86
  24.1 12.7 %collective-permute-start.2 = (bf16[2,208,256]{2,1,0:T(8,128)(2,1)}, bf16[2,208,256]{2,1,0:T(8,128)(2,1)S(1)}, u32[]{:S(2)}, u32[]{:S(2)}) collective-permute-start(bf16[2,208,256]{2,1,0:T(8,128)(2,1)} %get-tuple-element.17), channel_id=1, source_target_pairs={{16,32},{32,16},{48,64},{64,48},{80,96},{96,80},{112,128},{128,112... | collective-permute-start | bytes 638984 | tf_op jit(solution)/shard_map/ppermute | solution.py:351
  36.8 1.9 %collective-permute-start.3 = (bf16[2,208,256]{2,1,0:T(8,128)(2,1)}, bf16[2,208,256]{2,1,0:T(8,128)(2,1)S(1)}, u32[]{:S(2)}, u32[]{:S(2)}) collective-permute-start(bf16[2,208,256]{2,1,0:T(8,128)(2,1)} %get-tuple-element.18), channel_id=1, source_target_pairs={{0,16},{16,0},{32,48},{48,32},{64,80},{80,64},{96,112},{112,96},{1... | collective-permute-start | bytes 638984 | tf_op jit(solution)/shard_map/ppermute | solution.py:351
  38.7 0.0 copy-done
  38.7 0.0 copy-done.1
  38.8 0.0 copy-done.4
  38.8 0.0 copy-done.5
  38.8 0.0 copy-done.6
  38.8 0.0 copy-done.7
  38.8 0.0 copy-done.8
  38.8 0.0 copy-done.9
  38.8 0.0 copy-done.10
  38.8 0.0 copy-done.11
  38.8 0.0 copy-done.12
  38.8 0.0 copy-start.2
  38.9 0.7 %copy-done.2 = bf16[2,32,256]{2,1,0:T(8,128)(2,1)S(1)} copy-done((bf16[2,32,256]{2,1,0:T(8,128)(2,1)S(1)}, bf16[2,32,256]{2,1,0:T(8,128)(2,1)}, u32[]{:S(2)}) %copy-start.2) | copy-done | bytes 32792
  39.6 0.0 copy-start.3
  39.6 0.8 %copy-done.3 = bf16[2,32,256]{2,1,0:T(8,128)(2,1)S(1)} copy-done((bf16[2,32,256]{2,1,0:T(8,128)(2,1)S(1)}, bf16[2,32,256]{2,1,0:T(8,128)(2,1)}, u32[]{:S(2)}) %copy-start.3) | copy-done | bytes 32792
  40.4 8.7 %middle.1 = (bf16[1,16,96,256]{3,2,1,0:T(8,128)(2,1)}, bf16[3,4,96,256]{3,2,1,0:T(8,128)(2,1)S(1)}) custom-call(f32[32]{0:T(128)S(1)} %copy-done.9, f32[32]{0:T(128)S(1)} %copy-done.10, f32[32]{0:T(128)S(1)} %copy-done.11, f32[32]{0:T(128)S(1)} %copy-done.12, f32[1,256]{1,0:T(1,128)S(1)} %bitcast.5, f32[1,256]{1,0:T(1,128)S(1)} %bitcast.7, ...), custom_call_target="tpu_custom_call" | custom-call | tf_op jit(solution)/shard_map/middle/pallas_call | solution.py:217
  49.0 0.0 collective-permute-done.2.odd
  49.0 0.0 collective-permute-done.3.even
  49.0 5.4 %border.1 = bf16[1,16,96,256]{3,2,1,0:T(8,128)(2,1)} custom-call(f32[32]{0:T(128)S(1)} %copy-done.9, f32[32]{0:T(128)S(1)} %copy-done.10, f32[32]{0:T(128)S(1)} %copy-done.11, f32[32]{0:T(128)S(1)} %copy-done.12, f32[1,256]{1,0:T(1,128)S(1)} %bitcast.6, f32[1,256]{1,0:T(1,128)S(1)} %bitcast.8, ...), custom_call_target="tpu_custom_call", output_to_operand_aliasing={{}: (18, {})} | custom-call | tf_op jit(solution)/shard_map/border/pallas_call | solution.py:305
Async XLA Ops:
  1.6 37.1 %copy-start = (bf16[1,16,96,256]{3,2,1,0:T(8,128)(2,1)S(1)}, bf16[1,16,96,256]{3,2,1,0:T(8,128)(2,1)}, u32[]{:S(2)}) copy-start(bf16[1,16,96,256]{3,2,1,0:T(8,128)(2,1)} %img.7) | copy-start | bytes 2359300
  1.6 37.1 %copy-start.1 = (bf16[1,16,96,256]{3,2,1,0:T(8,128)(2,1)S(1)}, bf16[1,16,96,256]{3,2,1,0:T(8,128)(2,1)}, u32[]{:S(2)}) copy-start(bf16[1,16,96,256]{3,2,1,0:T(8,128)(2,1)} %cot.7) | copy-start | bytes 2359300
  1.6 37.1 %copy-start.4 = (f32[256]{0:T(256)S(1)}, f32[256]{0:T(256)}, u32[]{:S(2)}) copy-start(f32[256]{0:T(256)} %param.16) | copy-start | bytes 3076
  1.7 37.1 %copy-start.5 = (f32[256]{0:T(256)S(1)}, f32[256]{0:T(256)}, u32[]{:S(2)}) copy-start(f32[256]{0:T(256)} %param.20) | copy-start | bytes 3076
  1.7 37.1 %copy-start.6 = (f32[256]{0:T(256)S(1)}, f32[256]{0:T(256)}, u32[]{:S(2)}) copy-start(f32[256]{0:T(256)} %param.21) | copy-start | bytes 3076
  1.7 37.1 %copy-start.7 = (f32[256]{0:T(256)S(1)}, f32[256]{0:T(256)}, u32[]{:S(2)}) copy-start(f32[256]{0:T(256)} %param.24) | copy-start | bytes 3076
  1.7 37.1 %copy-start.8 = (f32[256]{0:T(256)S(1)}, f32[256]{0:T(256)}, u32[]{:S(2)}) copy-start(f32[256]{0:T(256)} %param.25) | copy-start | bytes 3076
  1.7 37.1 %copy-start.9 = (f32[32]{0:T(128)S(1)}, f32[32]{0:T(128)}, u32[]{:S(2)}) copy-start(f32[32]{0:T(128)} %stats_0_.3) | copy-start | bytes 388
  1.7 37.1 %copy-start.10 = (f32[32]{0:T(128)S(1)}, f32[32]{0:T(128)}, u32[]{:S(2)}) copy-start(f32[32]{0:T(128)} %stats_1_.3) | copy-start | bytes 388
  1.7 37.1 %copy-start.11 = (f32[32]{0:T(128)S(1)}, f32[32]{0:T(128)}, u32[]{:S(2)}) copy-start(f32[32]{0:T(128)} %stats_2_.3) | copy-start | bytes 388
  1.7 37.1 %copy-start.12 = (f32[32]{0:T(128)S(1)}, f32[32]{0:T(128)}, u32[]{:S(2)}) copy-start(f32[32]{0:T(128)} %stats_3_.3) | copy-start | bytes 388
  1.8 17.7 %collective-permute-start = (bf16[2,32,256]{2,1,0:T(8,128)(2,1)}, bf16[2,32,256]{2,1,0:T(8,128)(2,1)S(1)}, u32[]{:S(2)}, u32[]{:S(2)}) collective-permute-start(bf16[2,32,256]{2,1,0:T(8,128)(2,1)} %get-tuple-element.13), channel_id=1, source_target_pairs={{0,1},{1,0},{2,3},{3,2},{4,5},{5,4},{6,7},{7,6},{8,9},{9,8},{10,11... | collective-permute-start | bytes 98312 | tf_op jit(solution)/shard_map/ppermute | solution.py:351
  4.5 16.8 %collective-permute-start.1 = (bf16[2,32,256]{2,1,0:T(8,128)(2,1)}, bf16[2,32,256]{2,1,0:T(8,128)(2,1)S(1)}, u32[]{:S(2)}, u32[]{:S(2)}) collective-permute-start(bf16[2,32,256]{2,1,0:T(8,128)(2,1)} %get-tuple-element.14), channel_id=1, source_target_pairs={{1,2},{2,1},{3,4},{4,3},{5,6},{6,5},{7,8},{8,7},{9,10},{10,9},{11,... | collective-permute-start | bytes 98312 | tf_op jit(solution)/shard_map/ppermute | solution.py:351
  19.5 1.8 %copy-start.13 = (bf16[2,32,256]{2,1,0:T(8,128)(2,1)}, bf16[2,32,256]{2,1,0:T(8,128)(2,1)S(1)}, u32[]{:S(2)}) copy-start(bf16[2,32,256]{2,1,0:T(8,128)(2,1)S(1)} %collective-permute-done.ce) | copy-start | bytes 98308
  21.3 0.6 %copy-start.14 = (bf16[2,32,256]{2,1,0:T(8,128)(2,1)}, bf16[2,32,256]{2,1,0:T(8,128)(2,1)S(1)}, u32[]{:S(2)}) copy-start(bf16[2,32,256]{2,1,0:T(8,128)(2,1)S(1)} %collective-permute-done.1.co) | copy-start | bytes 98308
  24.1 24.9 %collective-permute-start.2 = (bf16[2,208,256]{2,1,0:T(8,128)(2,1)}, bf16[2,208,256]{2,1,0:T(8,128)(2,1)S(1)}, u32[]{:S(2)}, u32[]{:S(2)}) collective-permute-start(bf16[2,208,256]{2,1,0:T(8,128)(2,1)} %get-tuple-element.17), channel_id=1, source_target_pairs={{16,32},{32,16},{48,64},{64,48},{80,96},{96,80},{112,128},{128,112... | collective-permute-start | bytes 638984 | tf_op jit(solution)/shard_map/ppermute | solution.py:351
  36.8 12.2 %collective-permute-start.3 = (bf16[2,208,256]{2,1,0:T(8,128)(2,1)}, bf16[2,208,256]{2,1,0:T(8,128)(2,1)S(1)}, u32[]{:S(2)}, u32[]{:S(2)}) collective-permute-start(bf16[2,208,256]{2,1,0:T(8,128)(2,1)} %get-tuple-element.18), channel_id=1, source_target_pairs={{0,16},{16,0},{32,48},{48,32},{64,80},{80,64},{96,112},{112,96},{1... | collective-permute-start | bytes 638984 | tf_op jit(solution)/shard_map/ppermute | solution.py:351
  38.8 0.8 %copy-start.2 = (bf16[2,32,256]{2,1,0:T(8,128)(2,1)S(1)}, bf16[2,32,256]{2,1,0:T(8,128)(2,1)}, u32[]{:S(2)}) copy-start(bf16[2,32,256]{2,1,0:T(8,128)(2,1)} %get-tuple-element.15.ce) | copy-start | bytes 98308
  39.6 0.8 %copy-start.3 = (bf16[2,32,256]{2,1,0:T(8,128)(2,1)S(1)}, bf16[2,32,256]{2,1,0:T(8,128)(2,1)}, u32[]{:S(2)}) copy-start(bf16[2,32,256]{2,1,0:T(8,128)(2,1)} %get-tuple-element.16.co) | copy-start | bytes 98308

commit v3 on v2

--- a/solution.py
+++ b/solution.py
@@ -9,7 +9,7 @@
 F32, BF16 = jnp.float32, jnp.bfloat16
 ROWS, COLS = "rows", "cols"
 VMEM, HBM, SMEM = (pl.BlockSpec(memory_space=m) for m in (pltpu.VMEM, pltpu.HBM, pltpu.SMEM))
-LIMIT = pltpu.CompilerParams(vmem_limit_bytes=40 << 20)
+SMALL, LARGE = (pltpu.CompilerParams(vmem_limit_bytes=n << 20) for n in (4, 20))
 
 
 def place():
@@ -55,17 +55,17 @@
             pltpu.VMEM((2, 2 * H, C), F32),
             pltpu.SemaphoreType.DMA((4,)),
         ],
+        compiler_params=SMALL,
         name="edges",
     )(img, cot)
 
 
-def messages_kernel(img, cot, ce, co, odd, even, near_own, far_own, buf):
+def messages_kernel(img, cot, ce, co, odd, even, buf):
     H, W = img.shape[1], img.shape[2]
     n, m = 2 * W, ce.shape[1]
     odd_row, _, _ = place()
     buf[8:16] = jnp.zeros_like(buf[8:16])
     for k in range(2):
-        near_own[k], far_own[k] = ce[k], co[k]
         x = (img, cot)[k]
         for h in range(2):
             upper, lower = x[0, h], x[0, H - 2 + h]
@@ -81,14 +81,15 @@
 
 
 def messages(img, cot, ce, co):
-    n, m, C = 2 * img.shape[2], ce.shape[1], ce.shape[2]
+    n, C = 2 * img.shape[2], ce.shape[2]
     shape = lambda n: jax.ShapeDtypeStruct((2, n, C), BF16)
     return pl.pallas_call(
         messages_kernel,
-        out_shape=(shape(n + 16), shape(n + 16), shape(m), shape(m)),
+        out_shape=(shape(n + 16), shape(n + 16)),
         in_specs=[VMEM] * 4,
-        out_specs=(VMEM,) * 4,
+        out_specs=(VMEM,) * 2,
         scratch_shapes=[pltpu.VMEM((16, C), F32)],
+        compiler_params=SMALL,
         name="messages",
     )(img, cot, ce, co)
 
@@ -164,12 +165,9 @@
 
 
 def middle_kernel(
-    stats, vecs, img, cot, ce, co, w1, w2, out, kept, rowbuf, act3, cot3, in3, res, nbuf, fbuf, k1, k2, sems
+    stats, vecs, img, cot, ce, co, k1, k2, out, kept, rowbuf, act3, cot3, in3, res, nbuf, fbuf, sems
 ):
     H, W, C = img.shape[1:]
-    loads = [pltpu.make_async_copy(w1, k1, sems.at[0]), pltpu.make_async_copy(w2, k2, sems.at[1])]
-    for load in loads:
-        load.start()
     half_one, bias_one, half_two, bias_two = affine(stats, vecs, C)
     odd_row, odd_col, (up, down, to_left, to_right) = place()
     for k in range(2):
@@ -186,8 +184,6 @@
                 lft, rgt = act_of(lft, half_one, bias_one) * to_left, act_of(rgt, half_one, bias_one) * to_right
             fill(rowbuf.at[count % 4], own, lft, rgt, dst, h)
             count += 1
-    for load in loads:
-        load.wait()
     cmask = col_mask(to_left, to_right, W)
     R = (H - 2) // 2
     for b in range(0, H - 2, R):
@@ -217,7 +213,7 @@
     return pl.pallas_call(
         middle_kernel,
         out_shape=(jax.ShapeDtypeStruct(img.shape, BF16), jax.ShapeDtypeStruct((3, 4, W, C), BF16)),
-        in_specs=[(SMEM,) * 4, (VMEM,) * 5] + [VMEM] * 4 + [HBM, HBM],
+        in_specs=[(SMEM,) * 4, (VMEM,) * 5] + [VMEM] * 6,
         out_specs=(HBM, VMEM),
         scratch_shapes=[
             pltpu.VMEM((4, PADW + 16, C), F32),
@@ -227,24 +223,19 @@
             pltpu.VMEM((H - 4, W, C), BF16),
             pltpu.VMEM((2, 2 * H, C), F32),
             pltpu.VMEM((2, 2 * H, C), F32),
-            pltpu.VMEM(k1.shape, BF16),
-            pltpu.VMEM(k2.shape, BF16),
             pltpu.SemaphoreType.DMA((4,)),
         ],
-        compiler_params=LIMIT,
+        compiler_params=LARGE,
         name="middle",
     )(stats, vecs, img, cot, ce, co, k1, k2)
 
 
 def border_kernel(
-    stats, vecs, img, cot, ce, co, odd, even, w1, w2, kept, old, out,
-    rowbuf, act3, cot3, in3, res, nbuf, fbuf, k1, k2, sems,
+    stats, vecs, img, cot, ce, co, odd, even, k1, k2, kept, old, out,
+    rowbuf, act3, cot3, in3, res, nbuf, fbuf, sems,
 ):
     H, W, C = img.shape[1:]
     m = 2 * H
-    loads = [pltpu.make_async_copy(w1, k1, sems.at[0]), pltpu.make_async_copy(w2, k2, sems.at[1])]
-    for load in loads:
-        load.start()
     half_one, bias_one, half_two, bias_two = affine(stats, vecs, C)
     odd_row, odd_col, (up, down, to_left, to_right) = place()
     for k in range(2):
@@ -279,8 +270,6 @@
     for j in range(3):
         for s, d in enumerate((2, 3, 4, 5)):
             in3[j, d] = kept[j, s]
-    for load in loads:
-        load.wait()
     cmask = col_mask(to_left, to_right, W)
     c1 = conv(act3, k1, (0, 4), 2, PADW, False)
     c2 = conv(cot3, k2, (0, 4), 2, PADW, True)
@@ -305,7 +294,7 @@
     return pl.pallas_call(
         border_kernel,
         out_shape=jax.ShapeDtypeStruct(img.shape, BF16),
-        in_specs=[(SMEM,) * 4, (VMEM,) * 5] + [VMEM] * 6 + [HBM, HBM, VMEM, HBM],
+        in_specs=[(SMEM,) * 4, (VMEM,) * 5] + [VMEM] * 9 + [HBM],
         out_specs=HBM,
         input_output_aliases={4 + 5 + 6 + 3: 0},
         scratch_shapes=[
@@ -316,11 +305,9 @@
             pltpu.VMEM((4, W, C), BF16),
             pltpu.VMEM((2, 2 * H + 8, C), F32),
             pltpu.VMEM((2, 2 * H + 8, C), F32),
-            pltpu.VMEM(k1.shape, BF16),
-            pltpu.VMEM(k2.shape, BF16),
             pltpu.SemaphoreType.DMA((4,)),
         ],
-        compiler_params=LIMIT,
+        compiler_params=LARGE,
         name="border",
     )(stats, vecs, img, cot, ce, co, odd, even, k1, k2, kept, old)
 
@@ -350,11 +337,9 @@
         axis = COLS if name[0] == "c" else ROWS
         return lax.ppermute(x, axis, swaps(lax.axis_size(axis), int(name[1] == "o")))
 
-    stay = lambda x: pltpu.with_memory_space_constraint(x, pltpu.HBM)
-    first_kernel, second_kernel = stay(first_kernel), stay(second_kernel)
     near, far = edges(image_in, cotangent)
     co, ce = send("co", far), send("ce", near)
-    odd, even, ce, co = messages(image_in, cotangent, ce, co)
+    odd, even = messages(image_in, cotangent, ce, co)
     odd, even = send("ro", odd), send("re", even)
     out, kept = middle(stats, vecs, image_in, cotangent, ce, co, first_kernel, second_kernel)
     return border(stats, vecs, image_in, cotangent, ce, co, odd, even, first_kernel, second_kernel, kept, out)

time: 54.9 us -> 50.2 us (0.914)
  Pallas kernels: 17.9 us -> 12.1 us
  local copies, waits for them, and re-layouts: 2.18 us -> 3.6 us
    pallas_call x1, Pallas kernels: 2.21 us -> 0.06 us  [messages(): pl.pallas_call(messages_kernel, out_shape=(shape(n + 16), shape(n + 16)),...]
    pallas_call x1, Pallas kernels: 1.62 us -> 0.15 us  [edges(): pl.pallas_call(edges_kernel, out_shape=(shape, shape), in_specs=[HBM, HBM...]
    unnamed x30, local copies, waits for them, and re-layouts: 2.18 us -> 3.6 us
    pallas_call x1, Pallas kernels: 5.38 us -> 4.08 us  [border(): pl.pallas_call(border_kernel, out_shape=jax.ShapeDtypeStruct(img.shape, B...]
    pallas_call x1, Pallas kernels: 8.66 us -> 7.82 us  [middle(): pl.pallas_call(middle_kernel, out_shape=(jax.ShapeDtypeStruct(img.shape,...]
where the time goes in v3:
time: 50.2 us; the launch traced here: 49.9 us
  starting transfers between devices  32.3 us (64%)
  Pallas kernels  12.1 us (24%)
  local copies, waits for them, and re-layouts  3.6 us (7%)
  waiting for transfers between devices  1.58 us (3%)
    ppermute x4, starting transfers between devices, send(): lax.ppermute(x, axis, swaps(lax.axis_size(axis), int(name[1] == 'o')))  32.3 us
    pallas_call x1, Pallas kernels, middle(): pl.pallas_call(middle_kernel, out_shape=(jax.ShapeDtypeStruct(img.shape,...  7.82 us
    pallas_call x1, Pallas kernels, border(): pl.pallas_call(border_kernel, out_shape=jax.ShapeDtypeStruct(img.shape, B...  4.08 us
    unnamed x30, local copies, waits for them, and re-layouts  3.6 us
    ppermute x4, waiting for transfers between devices, send(): lax.ppermute(x, axis, swaps(lax.axis_size(axis), int(name[1] == 'o')))  1.58 us
  transfers between devices with their start and end apart: 4, of which 1 were waited for; matrix products, arithmetic and copies ran while one was open for 0% of the time, Pallas kernels for 16%

profile of v3, /device:TPU:31, one launch (start us, length us, event | category | flops | bytes accessed | tf_op | source)
XLA Modules:
  0.0 49.9 jit_solution(6195309147994414518)
XLA Ops:
  0.0 0.0 copy-start
  0.0 1.1 %copy-done = bf16[1,16,96,256]{3,2,1,0:T(8,128)(2,1)S(1)} copy-done((bf16[1,16,96,256]{3,2,1,0:T(8,128)(2,1)S(1)}, bf16[1,16,96,256]{3,2,1,0:T(8,128)(2,1)}, u32[]{:S(2)}) %copy-start) | copy-done | bytes 786456
  1.1 0.0 copy-start.2
  1.1 1.1 %copy-done.2 = bf16[1,16,96,256]{3,2,1,0:T(8,128)(2,1)S(1)} copy-done((bf16[1,16,96,256]{3,2,1,0:T(8,128)(2,1)S(1)}, bf16[1,16,96,256]{3,2,1,0:T(8,128)(2,1)}, u32[]{:S(2)}) %copy-start.2) | copy-done | bytes 786456
  2.3 0.0 copy-start.4
  2.3 0.1 edges.1
  2.4 0.0 copy-start.1
  2.4 0.0 copy-start.3
  2.5 0.0 copy-start.6
  2.5 0.0 copy-start.7
  2.5 0.0 copy-start.8
  2.5 0.0 copy-start.9
  2.5 0.0 copy-start.10
  2.5 0.0 copy-start.11
  2.5 0.0 copy-start.12
  2.5 0.0 copy-start.13
  2.5 0.0 copy-start.14
  2.6 2.7 %collective-permute-start = (bf16[2,32,256]{2,1,0:T(8,128)(2,1)S(1)}, bf16[2,32,256]{2,1,0:T(8,128)(2,1)S(1)}, u32[]{:S(2)}, u32[]{:S(2)}) collective-permute-start(bf16[2,32,256]{2,1,0:T(8,128)(2,1)S(1)} %get-tuple-element.11), channel_id=1, source_target_pairs={{0,1},{1,0},{2,3},{3,2},{4,5},{5,4},{6,7},{7,6},{8,9},{9,8},{10,11... | collective-permute-start | bytes 98312 | tf_op jit(solution)/shard_map/ppermute | solution.py:338
  5.3 15.0 %collective-permute-start.1 = (bf16[2,32,256]{2,1,0:T(8,128)(2,1)S(1)}, bf16[2,32,256]{2,1,0:T(8,128)(2,1)S(1)}, u32[]{:S(2)}, u32[]{:S(2)}) collective-permute-start(bf16[2,32,256]{2,1,0:T(8,128)(2,1)S(1)} %get-tuple-element.12), channel_id=1, source_target_pairs={{1,2},{2,1},{3,4},{4,3},{5,6},{6,5},{7,8},{8,7},{9,10},{10,9},{11,... | collective-permute-start | bytes 98312 | tf_op jit(solution)/shard_map/ppermute | solution.py:338
  20.3 0.0 collective-permute-done.ce
  20.3 1.6 %collective-permute-done.1.co = bf16[2,32,256]{2,1,0:T(8,128)(2,1)S(1)} collective-permute-done((bf16[2,32,256]{2,1,0:T(8,128)(2,1)S(1)}, bf16[2,32,256]{2,1,0:T(8,128)(2,1)S(1)}, u32[]{:S(2)}, u32[]{:S(2)}) %collective-permute-start.1) | collective-permute-done | bytes 32800 | tf_op jit(solution)/shard_map/ppermute | solution.py:338
  21.9 0.1 messages.1
  21.9 12.7 %collective-permute-start.2 = (bf16[2,208,256]{2,1,0:T(8,128)(2,1)S(1)}, bf16[2,208,256]{2,1,0:T(8,128)(2,1)S(1)}, u32[]{:S(2)}, u32[]{:S(2)}) collective-permute-start(bf16[2,208,256]{2,1,0:T(8,128)(2,1)S(1)} %get-tuple-element.13), channel_id=1, source_target_pairs={{16,32},{32,16},{48,64},{64,48},{80,96},{96,80},{112,128},{128,112... | collective-permute-start | bytes 638984 | tf_op jit(solution)/shard_map/ppermute | solution.py:338
  34.7 1.9 %collective-permute-start.3 = (bf16[2,208,256]{2,1,0:T(8,128)(2,1)S(1)}, bf16[2,208,256]{2,1,0:T(8,128)(2,1)S(1)}, u32[]{:S(2)}, u32[]{:S(2)}) collective-permute-start(bf16[2,208,256]{2,1,0:T(8,128)(2,1)S(1)} %get-tuple-element.14), channel_id=1, source_target_pairs={{0,16},{16,0},{32,48},{48,32},{64,80},{80,64},{96,112},{112,96},{1... | collective-permute-start | bytes 638984 | tf_op jit(solution)/shard_map/ppermute | solution.py:338
  36.6 0.0 copy-done.4
  36.6 0.0 copy-done.1
  36.6 0.0 copy-done.3
  36.6 0.0 copy-done.6
  36.6 0.0 copy-done.7
  36.6 0.0 copy-done.8
  36.6 0.0 copy-done.9
  36.7 0.0 copy-done.10
  36.7 0.0 copy-done.11
  36.7 0.0 copy-done.12
  36.7 0.0 copy-done.13
  36.7 0.0 copy-done.14
  36.7 0.0 copy-start.5
  36.7 1.3 %copy-done.5 = bf16[3,3,256,256]{3,2,1,0:T(8,128)(2,1)S(1)} copy-done((bf16[3,3,256,256]{3,2,1,0:T(8,128)(2,1)S(1)}, bf16[3,3,256,256]{3,2,1,0:T(8,128)(2,1)}, u32[]{:S(2)}) %copy-start.5) | copy-done | bytes 1179672
  38.0 7.8 %middle.1 = (bf16[1,16,96,256]{3,2,1,0:T(8,128)(2,1)}, bf16[3,4,96,256]{3,2,1,0:T(8,128)(2,1)S(1)}) custom-call(f32[32]{0:T(128)S(1)} %copy-done.11, f32[32]{0:T(128)S(1)} %copy-done.12, f32[32]{0:T(128)S(1)} %copy-done.13, f32[32]{0:T(128)S(1)} %copy-done.14, f32[1,256]{1,0:T(1,128)S(1)} %bitcast.5, f32[1,256]{1,0:T(1,128)S(1)} %bitcast.7, ...), custom_call_target="tpu_custom_call" | custom-call | tf_op jit(solution)/shard_map/middle/pallas_call | solution.py:213
  45.8 0.0 collective-permute-done.2.odd
  45.8 0.0 collective-permute-done.3.even
  45.8 4.1 %border.1 = bf16[1,16,96,256]{3,2,1,0:T(8,128)(2,1)} custom-call(f32[32]{0:T(128)S(1)} %copy-done.11, f32[32]{0:T(128)S(1)} %copy-done.12, f32[32]{0:T(128)S(1)} %copy-done.13, f32[32]{0:T(128)S(1)} %copy-done.14, f32[1,256]{1,0:T(1,128)S(1)} %bitcast.6, f32[1,256]{1,0:T(1,128)S(1)} %bitcast.8, ...), custom_call_target="tpu_custom_call", output_to_operand_aliasing={{}: (18, {})} | custom-call | tf_op jit(solution)/shard_map/border/pallas_call | solution.py:294
Async XLA Ops:
  0.0 1.1 %copy-start = (bf16[1,16,96,256]{3,2,1,0:T(8,128)(2,1)S(1)}, bf16[1,16,96,256]{3,2,1,0:T(8,128)(2,1)}, u32[]{:S(2)}) copy-start(bf16[1,16,96,256]{3,2,1,0:T(8,128)(2,1)} %img.7) | copy-start | bytes 2359300
  1.1 1.1 %copy-start.2 = (bf16[1,16,96,256]{3,2,1,0:T(8,128)(2,1)S(1)}, bf16[1,16,96,256]{3,2,1,0:T(8,128)(2,1)}, u32[]{:S(2)}) copy-start(bf16[1,16,96,256]{3,2,1,0:T(8,128)(2,1)} %cot.7) | copy-start | bytes 2359300
  2.3 34.3 %copy-start.4 = (bf16[3,3,256,256]{3,2,1,0:T(8,128)(2,1)S(1)}, bf16[3,3,256,256]{3,2,1,0:T(8,128)(2,1)}, u32[]{:S(2)}) copy-start(bf16[3,3,256,256]{3,2,1,0:T(8,128)(2,1)} %k1.3) | copy-start | bytes 3538948
  2.4 34.2 %copy-start.1 = (bf16[1,16,96,256]{3,2,1,0:T(8,128)(2,1)S(1)}, bf16[1,16,96,256]{3,2,1,0:T(8,128)(2,1)}, u32[]{:S(2)}) copy-start(bf16[1,16,96,256]{3,2,1,0:T(8,128)(2,1)} %img.7) | copy-start | bytes 2359300
  2.4 34.2 %copy-start.3 = (bf16[1,16,96,256]{3,2,1,0:T(8,128)(2,1)S(1)}, bf16[1,16,96,256]{3,2,1,0:T(8,128)(2,1)}, u32[]{:S(2)}) copy-start(bf16[1,16,96,256]{3,2,1,0:T(8,128)(2,1)} %cot.7) | copy-start | bytes 2359300
  2.5 34.2 %copy-start.6 = (f32[256]{0:T(256)S(1)}, f32[256]{0:T(256)}, u32[]{:S(2)}) copy-start(f32[256]{0:T(256)} %param.16) | copy-start | bytes 3076
  2.5 34.2 %copy-start.7 = (f32[256]{0:T(256)S(1)}, f32[256]{0:T(256)}, u32[]{:S(2)}) copy-start(f32[256]{0:T(256)} %param.20) | copy-start | bytes 3076
  2.5 34.2 %copy-start.8 = (f32[256]{0:T(256)S(1)}, f32[256]{0:T(256)}, u32[]{:S(2)}) copy-start(f32[256]{0:T(256)} %param.21) | copy-start | bytes 3076
  2.5 34.2 %copy-start.9 = (f32[256]{0:T(256)S(1)}, f32[256]{0:T(256)}, u32[]{:S(2)}) copy-start(f32[256]{0:T(256)} %param.24) | copy-start | bytes 3076
  2.5 34.2 %copy-start.10 = (f32[256]{0:T(256)S(1)}, f32[256]{0:T(256)}, u32[]{:S(2)}) copy-start(f32[256]{0:T(256)} %param.25) | copy-start | bytes 3076
  2.5 34.2 %copy-start.11 = (f32[32]{0:T(128)S(1)}, f32[32]{0:T(128)}, u32[]{:S(2)}) copy-start(f32[32]{0:T(128)} %stats_0_.3) | copy-start | bytes 388
  2.5 34.1 %copy-start.12 = (f32[32]{0:T(128)S(1)}, f32[32]{0:T(128)}, u32[]{:S(2)}) copy-start(f32[32]{0:T(128)} %stats_1_.3) | copy-start | bytes 388
  2.5 34.1 %copy-start.13 = (f32[32]{0:T(128)S(1)}, f32[32]{0:T(128)}, u32[]{:S(2)}) copy-start(f32[32]{0:T(128)} %stats_2_.3) | copy-start | bytes 388
  2.5 34.1 %copy-start.14 = (f32[32]{0:T(128)S(1)}, f32[32]{0:T(128)}, u32[]{:S(2)}) copy-start(f32[32]{0:T(128)} %stats_3_.3) | copy-start | bytes 388
  2.6 17.7 %collective-permute-start = (bf16[2,32,256]{2,1,0:T(8,128)(2,1)S(1)}, bf16[2,32,256]{2,1,0:T(8,128)(2,1)S(1)}, u32[]{:S(2)}, u32[]{:S(2)}) collective-permute-start(bf16[2,32,256]{2,1,0:T(8,128)(2,1)S(1)} %get-tuple-element.11), channel_id=1, source_target_pairs={{0,1},{1,0},{2,3},{3,2},{4,5},{5,4},{6,7},{7,6},{8,9},{9,8},{10,11... | collective-permute-start | bytes 98312 | tf_op jit(solution)/shard_map/ppermute | solution.py:338
  5.3 16.6 %collective-permute-start.1 = (bf16[2,32,256]{2,1,0:T(8,128)(2,1)S(1)}, bf16[2,32,256]{2,1,0:T(8,128)(2,1)S(1)}, u32[]{:S(2)}, u32[]{:S(2)}) collective-permute-start(bf16[2,32,256]{2,1,0:T(8,128)(2,1)S(1)} %get-tuple-element.12), channel_id=1, source_target_pairs={{1,2},{2,1},{3,4},{4,3},{5,6},{6,5},{7,8},{8,7},{9,10},{10,9},{11,... | collective-permute-start | bytes 98312 | tf_op jit(solution)/shard_map/ppermute | solution.py:338
  21.9 23.9 %collective-permute-start.2 = (bf16[2,208,256]{2,1,0:T(8,128)(2,1)S(1)}, bf16[2,208,256]{2,1,0:T(8,128)(2,1)S(1)}, u32[]{:S(2)}, u32[]{:S(2)}) collective-permute-start(bf16[2,208,256]{2,1,0:T(8,128)(2,1)S(1)} %get-tuple-element.13), channel_id=1, source_target_pairs={{16,32},{32,16},{48,64},{64,48},{80,96},{96,80},{112,128},{128,112... | collective-permute-start | bytes 638984 | tf_op jit(solution)/shard_map/ppermute | solution.py:338
  34.7 11.2 %collective-permute-start.3 = (bf16[2,208,256]{2,1,0:T(8,128)(2,1)S(1)}, bf16[2,208,256]{2,1,0:T(8,128)(2,1)S(1)}, u32[]{:S(2)}, u32[]{:S(2)}) collective-permute-start(bf16[2,208,256]{2,1,0:T(8,128)(2,1)S(1)} %get-tuple-element.14), channel_id=1, source_target_pairs={{0,16},{16,0},{32,48},{48,32},{64,80},{80,64},{96,112},{112,96},{1... | collective-permute-start | bytes 638984 | tf_op jit(solution)/shard_map/ppermute | solution.py:338
  36.7 1.3 %copy-start.5 = (bf16[3,3,256,256]{3,2,1,0:T(8,128)(2,1)S(1)}, bf16[3,3,256,256]{3,2,1,0:T(8,128)(2,1)}, u32[]{:S(2)}) copy-start(bf16[3,3,256,256]{3,2,1,0:T(8,128)(2,1)} %k2.3) | copy-start | bytes 3538948

commit v4 on v3

--- a/solution.py
+++ b/solution.py
@@ -165,9 +165,11 @@
 
 
 def middle_kernel(
-    stats, vecs, img, cot, ce, co, k1, k2, out, kept, rowbuf, act3, cot3, in3, res, nbuf, fbuf, sems
+    stats, vecs, img, cot, ce, co, k1, w2, out, kept, rowbuf, act3, cot3, in3, res, nbuf, fbuf, k2, sems
 ):
     H, W, C = img.shape[1:]
+    load = pltpu.make_async_copy(w2, k2, sems.at[0])
+    load.start()
     half_one, bias_one, half_two, bias_two = affine(stats, vecs, C)
     odd_row, odd_col, (up, down, to_left, to_right) = place()
     for k in range(2):
@@ -184,6 +186,7 @@
                 lft, rgt = act_of(lft, half_one, bias_one) * to_left, act_of(rgt, half_one, bias_one) * to_right
             fill(rowbuf.at[count % 4], own, lft, rgt, dst, h)
             count += 1
+    load.wait()
     cmask = col_mask(to_left, to_right, W)
     R = (H - 2) // 2
     for b in range(0, H - 2, R):
@@ -213,7 +216,7 @@
     return pl.pallas_call(
         middle_kernel,
         out_shape=(jax.ShapeDtypeStruct(img.shape, BF16), jax.ShapeDtypeStruct((3, 4, W, C), BF16)),
-        in_specs=[(SMEM,) * 4, (VMEM,) * 5] + [VMEM] * 6,
+        in_specs=[(SMEM,) * 4, (VMEM,) * 5] + [VMEM] * 5 + [HBM],
         out_specs=(HBM, VMEM),
         scratch_shapes=[
             pltpu.VMEM((4, PADW + 16, C), F32),
@@ -223,6 +226,7 @@
             pltpu.VMEM((H - 4, W, C), BF16),
             pltpu.VMEM((2, 2 * H, C), F32),
             pltpu.VMEM((2, 2 * H, C), F32),
+            pltpu.VMEM(k2.shape, BF16),
             pltpu.SemaphoreType.DMA((4,)),
         ],
         compiler_params=LARGE,
@@ -231,11 +235,13 @@
 
 
 def border_kernel(
-    stats, vecs, img, cot, ce, co, odd, even, k1, k2, kept, old, out,
-    rowbuf, act3, cot3, in3, res, nbuf, fbuf, sems,
+    stats, vecs, img, cot, ce, co, odd, even, k1, w2, kept, old, out,
+    rowbuf, act3, cot3, in3, res, nbuf, fbuf, k2, sems,
 ):
     H, W, C = img.shape[1:]
     m = 2 * H
+    load = pltpu.make_async_copy(w2, k2, sems.at[0])
+    load.start()
     half_one, bias_one, half_two, bias_two = affine(stats, vecs, C)
     odd_row, odd_col, (up, down, to_left, to_right) = place()
     for k in range(2):
@@ -270,6 +276,7 @@
     for j in range(3):
         for s, d in enumerate((2, 3, 4, 5)):
             in3[j, d] = kept[j, s]
+    load.wait()
     cmask = col_mask(to_left, to_right, W)
     c1 = conv(act3, k1, (0, 4), 2, PADW, False)
     c2 = conv(cot3, k2, (0, 4), 2, PADW, True)
@@ -294,7 +301,7 @@
     return pl.pallas_call(
         border_kernel,
         out_shape=jax.ShapeDtypeStruct(img.shape, BF16),
-        in_specs=[(SMEM,) * 4, (VMEM,) * 5] + [VMEM] * 9 + [HBM],
+        in_specs=[(SMEM,) * 4, (VMEM,) * 5] + [VMEM] * 7 + [HBM, VMEM, HBM],
         out_specs=HBM,
         input_output_aliases={4 + 5 + 6 + 3: 0},
         scratch_shapes=[
@@ -305,6 +312,7 @@
             pltpu.VMEM((4, W, C), BF16),
             pltpu.VMEM((2, 2 * H + 8, C), F32),
             pltpu.VMEM((2, 2 * H + 8, C), F32),
+            pltpu.VMEM(k2.shape, BF16),
             pltpu.SemaphoreType.DMA((4,)),
         ],
         compiler_params=LARGE,
@@ -337,7 +345,9 @@
         axis = COLS if name[0] == "c" else ROWS
         return lax.ppermute(x, axis, swaps(lax.axis_size(axis), int(name[1] == "o")))
 
-    near, far = edges(image_in, cotangent)
+    stay = lambda x: pltpu.with_memory_space_constraint(x, pltpu.HBM)
+    second_kernel = stay(second_kernel)
+    near, far = edges(stay(image_in), stay(cotangent))
     co, ce = send("co", far), send("ce", near)
     odd, even = messages(image_in, cotangent, ce, co)
     odd, even = send("ro", odd), send("re", even)

time: 50.2 us -> 49.4 us (0.984)
  local copies, waits for them, and re-layouts: 3.6 us -> 0.07 us
  Pallas kernels: 12.1 us -> 14.9 us
    unnamed x30 -> x24, local copies, waits for them, and re-layouts: 3.6 us -> 0.07 us
    pallas_call x1, Pallas kernels: 0.15 us -> 1.12 us  [edges(): pl.pallas_call(edges_kernel, out_shape=(shape, shape), in_specs=[HBM, HBM...]
    pallas_call x1, Pallas kernels: 4.08 us -> 5.04 us  [border(): pl.pallas_call(border_kernel, out_shape=jax.ShapeDtypeStruct(img.shape, B...]
    pallas_call x1, Pallas kernels: 7.82 us -> 8.71 us  [middle(): pl.pallas_call(middle_kernel, out_shape=(jax.ShapeDtypeStruct(img.shape,...]
  transfers between devices with their start and end apart: 4 -> 4, of which waited for: 1 -> 1; matrix products, arithmetic and copies ran while one was open for 0% -> 0% of each run, Pallas kernels for 16% -> 18%
where the time goes in v4:
time: 49.4 us; the launch traced here: 49.2 us
  starting transfers between devices  32.3 us (65%)
  Pallas kernels  14.9 us (30%)
  waiting for transfers between devices  1.58 us (3%)
    ppermute x4, starting transfers between devices, send(): lax.ppermute(x, axis, swaps(lax.axis_size(axis), int(name[1] == 'o')))  32.3 us
    pallas_call x1, Pallas kernels, middle(): pl.pallas_call(middle_kernel, out_shape=(jax.ShapeDtypeStruct(img.shape,...  8.71 us
    pallas_call x1, Pallas kernels, border(): pl.pallas_call(border_kernel, out_shape=jax.ShapeDtypeStruct(img.shape, B...  5.04 us
    ppermute x4, waiting for transfers between devices, send(): lax.ppermute(x, axis, swaps(lax.axis_size(axis), int(name[1] == 'o')))  1.58 us
    pallas_call x1, Pallas kernels, edges(): pl.pallas_call(edges_kernel, out_shape=(shape, shape), in_specs=[HBM, HBM...  1.12 us
  transfers between devices with their start and end apart: 4, of which 1 were waited for; matrix products, arithmetic and copies ran while one was open for 0% of the time, Pallas kernels for 18%

profile of v4, /device:TPU:31, one launch (start us, length us, event | category | flops | bytes accessed | tf_op | source)
XLA Modules:
  0.0 49.2 jit_solution(7811901557967704735)
XLA Ops:
  0.0 0.0 copy-start.1
  0.0 0.0 copy-start
  0.0 1.1 %edges.1 = (bf16[2,32,256]{2,1,0:T(8,128)(2,1)S(1)}, bf16[2,32,256]{2,1,0:T(8,128)(2,1)S(1)}) custom-call(bf16[1,16,96,256]{3,2,1,0:T(8,128)(2,1)} %img.7, bf16[1,16,96,256]{3,2,1,0:T(8,128)(2,1)} %cot.7), custom_call_target="tpu_custom_call" | custom-call | tf_op jit(solution)/shard_map/edges/pallas_call | solution.py:47
  1.1 0.0 copy-start.2
  1.1 0.0 copy-start.3
  1.2 0.0 copy-start.4
  1.2 0.0 copy-start.5
  1.2 0.0 copy-start.6
  1.2 0.0 copy-start.7
  1.2 0.0 copy-start.8
  1.2 0.0 copy-start.9
  1.2 0.0 copy-start.10
  1.2 0.0 copy-start.11
  1.3 2.7 %collective-permute-start = (bf16[2,32,256]{2,1,0:T(8,128)(2,1)S(1)}, bf16[2,32,256]{2,1,0:T(8,128)(2,1)S(1)}, u32[]{:S(2)}, u32[]{:S(2)}) collective-permute-start(bf16[2,32,256]{2,1,0:T(8,128)(2,1)S(1)} %get-tuple-element.11), channel_id=1, source_target_pairs={{0,1},{1,0},{2,3},{3,2},{4,5},{5,4},{6,7},{7,6},{8,9},{9,8},{10,11... | collective-permute-start | bytes 98312 | tf_op jit(solution)/shard_map/ppermute | solution.py:346
  4.0 15.0 %collective-permute-start.1 = (bf16[2,32,256]{2,1,0:T(8,128)(2,1)S(1)}, bf16[2,32,256]{2,1,0:T(8,128)(2,1)S(1)}, u32[]{:S(2)}, u32[]{:S(2)}) collective-permute-start(bf16[2,32,256]{2,1,0:T(8,128)(2,1)S(1)} %get-tuple-element.12), channel_id=1, source_target_pairs={{1,2},{2,1},{3,4},{4,3},{5,6},{6,5},{7,8},{8,7},{9,10},{10,9},{11,... | collective-permute-start | bytes 98312 | tf_op jit(solution)/shard_map/ppermute | solution.py:346
  19.0 0.0 collective-permute-done.ce
  19.0 1.6 %collective-permute-done.1.co = bf16[2,32,256]{2,1,0:T(8,128)(2,1)S(1)} collective-permute-done((bf16[2,32,256]{2,1,0:T(8,128)(2,1)S(1)}, bf16[2,32,256]{2,1,0:T(8,128)(2,1)S(1)}, u32[]{:S(2)}, u32[]{:S(2)}) %collective-permute-start.1) | collective-permute-done | bytes 32800 | tf_op jit(solution)/shard_map/ppermute | solution.py:346
  20.6 0.0 copy-done.1
  20.6 0.0 copy-done
  20.6 0.1 messages.1
  20.6 12.7 %collective-permute-start.2 = (bf16[2,208,256]{2,1,0:T(8,128)(2,1)S(1)}, bf16[2,208,256]{2,1,0:T(8,128)(2,1)S(1)}, u32[]{:S(2)}, u32[]{:S(2)}) collective-permute-start(bf16[2,208,256]{2,1,0:T(8,128)(2,1)S(1)} %get-tuple-element.13), channel_id=1, source_target_pairs={{16,32},{32,16},{48,64},{64,48},{80,96},{96,80},{112,128},{128,112... | collective-permute-start | bytes 638984 | tf_op jit(solution)/shard_map/ppermute | solution.py:346
  33.4 1.9 %collective-permute-start.3 = (bf16[2,208,256]{2,1,0:T(8,128)(2,1)S(1)}, bf16[2,208,256]{2,1,0:T(8,128)(2,1)S(1)}, u32[]{:S(2)}, u32[]{:S(2)}) collective-permute-start(bf16[2,208,256]{2,1,0:T(8,128)(2,1)S(1)} %get-tuple-element.14), channel_id=1, source_target_pairs={{0,16},{16,0},{32,48},{48,32},{64,80},{80,64},{96,112},{112,96},{1... | collective-permute-start | bytes 638984 | tf_op jit(solution)/shard_map/ppermute | solution.py:346
  35.3 0.0 copy-done.2
  35.3 0.0 copy-done.3
  35.3 0.0 copy-done.4
  35.3 0.0 copy-done.5
  35.3 0.0 copy-done.6
  35.3 0.0 copy-done.7
  35.3 0.0 copy-done.8
  35.4 0.0 copy-done.9
  35.4 0.0 copy-done.10
  35.4 0.0 copy-done.11
  35.4 8.7 %middle.1 = (bf16[1,16,96,256]{3,2,1,0:T(8,128)(2,1)}, bf16[3,4,96,256]{3,2,1,0:T(8,128)(2,1)S(1)}) custom-call(f32[32]{0:T(128)S(1)} %copy-done.8, f32[32]{0:T(128)S(1)} %copy-done.9, f32[32]{0:T(128)S(1)} %copy-done.10, f32[32]{0:T(128)S(1)} %copy-done.11, f32[1,256]{1,0:T(1,128)S(1)} %bitcast.5, f32[1,256]{1,0:T(1,128)S(1)} %bitcast.7, ...), custom_call_target="tpu_custom_call" | custom-call | tf_op jit(solution)/shard_map/middle/pallas_call | solution.py:216
  44.1 0.0 collective-permute-done.2.odd
  44.1 0.0 collective-permute-done.3.even
  44.1 5.0 %border.1 = bf16[1,16,96,256]{3,2,1,0:T(8,128)(2,1)} custom-call(f32[32]{0:T(128)S(1)} %copy-done.8, f32[32]{0:T(128)S(1)} %copy-done.9, f32[32]{0:T(128)S(1)} %copy-done.10, f32[32]{0:T(128)S(1)} %copy-done.11, f32[1,256]{1,0:T(1,128)S(1)} %bitcast.6, f32[1,256]{1,0:T(1,128)S(1)} %bitcast.8, ...), custom_call_target="tpu_custom_call", output_to_operand_aliasing={{}: (18, {})} | custom-call | tf_op jit(solution)/shard_map/border/pallas_call | solution.py:301
Async XLA Ops:
  0.0 20.6 %copy-start.1 = (bf16[1,16,96,256]{3,2,1,0:T(8,128)(2,1)S(1)}, bf16[1,16,96,256]{3,2,1,0:T(8,128)(2,1)}, u32[]{:S(2)}) copy-start(bf16[1,16,96,256]{3,2,1,0:T(8,128)(2,1)} %cot.7) | copy-start | bytes 2359300
  0.0 20.6 %copy-start = (bf16[1,16,96,256]{3,2,1,0:T(8,128)(2,1)S(1)}, bf16[1,16,96,256]{3,2,1,0:T(8,128)(2,1)}, u32[]{:S(2)}) copy-start(bf16[1,16,96,256]{3,2,1,0:T(8,128)(2,1)} %img.7) | copy-start | bytes 2359300
  1.1 34.2 %copy-start.2 = (bf16[3,3,256,256]{3,2,1,0:T(8,128)(2,1)S(1)}, bf16[3,3,256,256]{3,2,1,0:T(8,128)(2,1)}, u32[]{:S(2)}) copy-start(bf16[3,3,256,256]{3,2,1,0:T(8,128)(2,1)} %k1.3) | copy-start | bytes 3538948
  1.1 34.1 %copy-start.3 = (f32[256]{0:T(256)S(1)}, f32[256]{0:T(256)}, u32[]{:S(2)}) copy-start(f32[256]{0:T(256)} %param.16) | copy-start | bytes 3076
  1.2 34.1 %copy-start.4 = (f32[256]{0:T(256)S(1)}, f32[256]{0:T(256)}, u32[]{:S(2)}) copy-start(f32[256]{0:T(256)} %param.20) | copy-start | bytes 3076
  1.2 34.1 %copy-start.5 = (f32[256]{0:T(256)S(1)}, f32[256]{0:T(256)}, u32[]{:S(2)}) copy-start(f32[256]{0:T(256)} %param.21) | copy-start | bytes 3076
  1.2 34.1 %copy-start.6 = (f32[256]{0:T(256)S(1)}, f32[256]{0:T(256)}, u32[]{:S(2)}) copy-start(f32[256]{0:T(256)} %param.24) | copy-start | bytes 3076
  1.2 34.1 %copy-start.7 = (f32[256]{0:T(256)S(1)}, f32[256]{0:T(256)}, u32[]{:S(2)}) copy-start(f32[256]{0:T(256)} %param.25) | copy-start | bytes 3076
  1.2 34.1 %copy-start.8 = (f32[32]{0:T(128)S(1)}, f32[32]{0:T(128)}, u32[]{:S(2)}) copy-start(f32[32]{0:T(128)} %stats_0_.3) | copy-start | bytes 388
  1.2 34.1 %copy-start.9 = (f32[32]{0:T(128)S(1)}, f32[32]{0:T(128)}, u32[]{:S(2)}) copy-start(f32[32]{0:T(128)} %stats_1_.3) | copy-start | bytes 388
  1.2 34.1 %copy-start.10 = (f32[32]{0:T(128)S(1)}, f32[32]{0:T(128)}, u32[]{:S(2)}) copy-start(f32[32]{0:T(128)} %stats_2_.3) | copy-start | bytes 388
  1.2 34.1 %copy-start.11 = (f32[32]{0:T(128)S(1)}, f32[32]{0:T(128)}, u32[]{:S(2)}) copy-start(f32[32]{0:T(128)} %stats_3_.3) | copy-start | bytes 388
  1.3 17.7 %collective-permute-start = (bf16[2,32,256]{2,1,0:T(8,128)(2,1)S(1)}, bf16[2,32,256]{2,1,0:T(8,128)(2,1)S(1)}, u32[]{:S(2)}, u32[]{:S(2)}) collective-permute-start(bf16[2,32,256]{2,1,0:T(8,128)(2,1)S(1)} %get-tuple-element.11), channel_id=1, source_target_pairs={{0,1},{1,0},{2,3},{3,2},{4,5},{5,4},{6,7},{7,6},{8,9},{9,8},{10,11... | collective-permute-start | bytes 98312 | tf_op jit(solution)/shard_map/ppermute | solution.py:346
  4.0 16.6 %collective-permute-start.1 = (bf16[2,32,256]{2,1,0:T(8,128)(2,1)S(1)}, bf16[2,32,256]{2,1,0:T(8,128)(2,1)S(1)}, u32[]{:S(2)}, u32[]{:S(2)}) collective-permute-start(bf16[2,32,256]{2,1,0:T(8,128)(2,1)S(1)} %get-tuple-element.12), channel_id=1, source_target_pairs={{1,2},{2,1},{3,4},{4,3},{5,6},{6,5},{7,8},{8,7},{9,10},{10,9},{11,... | collective-permute-start | bytes 98312 | tf_op jit(solution)/shard_map/ppermute | solution.py:346
  20.6 23.5 %collective-permute-start.2 = (bf16[2,208,256]{2,1,0:T(8,128)(2,1)S(1)}, bf16[2,208,256]{2,1,0:T(8,128)(2,1)S(1)}, u32[]{:S(2)}, u32[]{:S(2)}) collective-permute-start(bf16[2,208,256]{2,1,0:T(8,128)(2,1)S(1)} %get-tuple-element.13), channel_id=1, source_target_pairs={{16,32},{32,16},{48,64},{64,48},{80,96},{96,80},{112,128},{128,112... | collective-permute-start | bytes 638984 | tf_op jit(solution)/shard_map/ppermute | solution.py:346
  33.4 10.8 %collective-permute-start.3 = (bf16[2,208,256]{2,1,0:T(8,128)(2,1)S(1)}, bf16[2,208,256]{2,1,0:T(8,128)(2,1)S(1)}, u32[]{:S(2)}, u32[]{:S(2)}) collective-permute-start(bf16[2,208,256]{2,1,0:T(8,128)(2,1)S(1)} %get-tuple-element.14), channel_id=1, source_target_pairs={{0,16},{16,0},{32,48},{48,32},{64,80},{80,64},{96,112},{112,96},{1... | collective-permute-start | bytes 638984 | tf_op jit(solution)/shard_map/ppermute | solution.py:346

commit v5 on v4

--- a/solution.py
+++ b/solution.py
@@ -174,27 +174,31 @@
     odd_row, odd_col, (up, down, to_left, to_right) = place()
     for k in range(2):
         nbuf[k], fbuf[k] = ce[k].astype(F32), co[k].astype(F32)
-    count = 0
-    for h in range(H):
-        for k, (src, dst) in enumerate(((img, act3), (cot, cot3))):
-            cut = slice(2 * h, 2 * h + 2)
-            near, far = nbuf[k, cut], fbuf[k, cut]
-            lft, rgt = jnp.where(odd_col, near, far), jnp.where(odd_col, far, near)
-            own = src[0, h]
-            if k == 0:
-                own = act_of(own, half_one, bias_one)
-                lft, rgt = act_of(lft, half_one, bias_one) * to_left, act_of(rgt, half_one, bias_one) * to_right
-            fill(rowbuf.at[count % 4], own, lft, rgt, dst, h)
-            count += 1
-    load.wait()
+
+    def prepare(rows):
+        for h in rows:
+            for k, (src, dst) in enumerate(((img, act3), (cot, cot3))):
+                cut = slice(2 * h, 2 * h + 2)
+                near, far = nbuf[k, cut], fbuf[k, cut]
+                lft, rgt = jnp.where(odd_col, near, far), jnp.where(odd_col, far, near)
+                own = src[0, h]
+                if k == 0:
+                    own = act_of(own, half_one, bias_one)
+                    lft, rgt = act_of(lft, half_one, bias_one) * to_left, act_of(rgt, half_one, bias_one) * to_right
+                fill(rowbuf.at[(2 * h + k) % 4], own, lft, rgt, dst, h)
+
     cmask = col_mask(to_left, to_right, W)
     R = (H - 2) // 2
+    prepare(range(R + 2))
+    load.wait()
     for b in range(0, H - 2, R):
         c1 = conv(act3, k1, (b,), R, PADW, False)
+        if b == 0:
+            prepare(range(R + 2, H))
         c2 = conv(cot3, k2, (b,), R, PADW, True)
         for r in range(R):
             g = inner_rows(c1, c2, r, half_two, bias_two, cmask)
-            store_inner(rowbuf.at[r % 4], g, in3, b + r, W)
+            store_inner(rowbuf.at[4 + r % 4], g, in3, b + r, W)
     for j in range(3):
         for s, h in enumerate((0, 1, H - 4, H - 3)):
             kept[j, s] = in3[j, h]
@@ -219,7 +223,7 @@
         in_specs=[(SMEM,) * 4, (VMEM,) * 5] + [VMEM] * 5 + [HBM],
         out_specs=(HBM, VMEM),
         scratch_shapes=[
-            pltpu.VMEM((4, PADW + 16, C), F32),
+            pltpu.VMEM((8, PADW + 16, C), F32),
             pltpu.VMEM((3, H, PADW, C), BF16),
             pltpu.VMEM((3, H, PADW, C), BF16),
             pltpu.VMEM((3, H - 2, W, C), BF16),
@@ -341,6 +345,7 @@
 ):
     stats = (first_center, first_inverse, second_center, second_inverse)
     vecs = tuple(v[None] for v in (first_bias, first_gain, first_shift, second_gain, second_shift))
+
     def send(name, x):
         axis = COLS if name[0] == "c" else ROWS
         return lax.ppermute(x, axis, swaps(lax.axis_size(axis), int(name[1] == "o")))

time: 49.4 us -> 49.4 us (level)
  no operation moved by 1% of the time
where the time goes in v5:
time: 49.4 us; the launch traced here: 49.1 us
  starting transfers between devices  32.3 us (65%)
  Pallas kernels  14.9 us (30%)
  waiting for transfers between devices  1.58 us (3%)
    ppermute x4, starting transfers between devices, send(): lax.ppermute(x, axis, swaps(lax.axis_size(axis), int(name[1] == 'o')))  32.3 us
    pallas_call x1, Pallas kernels, middle(): pl.pallas_call(middle_kernel, out_shape=(jax.ShapeDtypeStruct(img.shape,...  8.67 us
    pallas_call x1, Pallas kernels, border(): pl.pallas_call(border_kernel, out_shape=jax.ShapeDtypeStruct(img.shape, B...  5.04 us
    ppermute x4, waiting for transfers between devices, send(): lax.ppermute(x, axis, swaps(lax.axis_size(axis), int(name[1] == 'o')))  1.58 us
    pallas_call x1, Pallas kernels, edges(): pl.pallas_call(edges_kernel, out_shape=(shape, shape), in_specs=[HBM, HBM...  1.12 us
  transfers between devices with their start and end apart: 4, of which 1 were waited for; matrix products, arithmetic and copies ran while one was open for 0% of the time, Pallas kernels for 18%

profile of v5, /device:TPU:31, one launch (start us, length us, event | category | flops | bytes accessed | tf_op | source)
XLA Modules:
  0.0 49.1 jit_solution(13100125633263043668)
XLA Ops:
  0.0 0.0 copy-start.1
  0.0 0.0 copy-start
  0.0 1.1 %edges.1 = (bf16[2,32,256]{2,1,0:T(8,128)(2,1)S(1)}, bf16[2,32,256]{2,1,0:T(8,128)(2,1)S(1)}) custom-call(bf16[1,16,96,256]{3,2,1,0:T(8,128)(2,1)} %img.7, bf16[1,16,96,256]{3,2,1,0:T(8,128)(2,1)} %cot.7), custom_call_target="tpu_custom_call" | custom-call | tf_op jit(solution)/shard_map/edges/pallas_call | solution.py:47
  1.1 0.0 copy-start.2
  1.1 0.0 copy-start.3
  1.2 0.0 copy-start.4
  1.2 0.0 copy-start.5
  1.2 0.0 copy-start.6
  1.2 0.0 copy-start.7
  1.2 0.0 copy-start.8
  1.2 0.0 copy-start.9
  1.2 0.0 copy-start.10
  1.2 0.0 copy-start.11
  1.3 2.7 %collective-permute-start = (bf16[2,32,256]{2,1,0:T(8,128)(2,1)S(1)}, bf16[2,32,256]{2,1,0:T(8,128)(2,1)S(1)}, u32[]{:S(2)}, u32[]{:S(2)}) collective-permute-start(bf16[2,32,256]{2,1,0:T(8,128)(2,1)S(1)} %get-tuple-element.11), channel_id=1, source_target_pairs={{0,1},{1,0},{2,3},{3,2},{4,5},{5,4},{6,7},{7,6},{8,9},{9,8},{10,11... | collective-permute-start | bytes 98312 | tf_op jit(solution)/shard_map/ppermute | solution.py:351
  4.0 15.0 %collective-permute-start.1 = (bf16[2,32,256]{2,1,0:T(8,128)(2,1)S(1)}, bf16[2,32,256]{2,1,0:T(8,128)(2,1)S(1)}, u32[]{:S(2)}, u32[]{:S(2)}) collective-permute-start(bf16[2,32,256]{2,1,0:T(8,128)(2,1)S(1)} %get-tuple-element.12), channel_id=1, source_target_pairs={{1,2},{2,1},{3,4},{4,3},{5,6},{6,5},{7,8},{8,7},{9,10},{10,9},{11,... | collective-permute-start | bytes 98312 | tf_op jit(solution)/shard_map/ppermute | solution.py:351
  19.0 0.0 collective-permute-done.ce
  19.0 1.6 %collective-permute-done.1.co = bf16[2,32,256]{2,1,0:T(8,128)(2,1)S(1)} collective-permute-done((bf16[2,32,256]{2,1,0:T(8,128)(2,1)S(1)}, bf16[2,32,256]{2,1,0:T(8,128)(2,1)S(1)}, u32[]{:S(2)}, u32[]{:S(2)}) %collective-permute-start.1) | collective-permute-done | bytes 32800 | tf_op jit(solution)/shard_map/ppermute | solution.py:351
  20.6 0.0 copy-done.1
  20.6 0.0 copy-done
  20.6 0.1 messages.1
  20.6 12.7 %collective-permute-start.2 = (bf16[2,208,256]{2,1,0:T(8,128)(2,1)S(1)}, bf16[2,208,256]{2,1,0:T(8,128)(2,1)S(1)}, u32[]{:S(2)}, u32[]{:S(2)}) collective-permute-start(bf16[2,208,256]{2,1,0:T(8,128)(2,1)S(1)} %get-tuple-element.13), channel_id=1, source_target_pairs={{16,32},{32,16},{48,64},{64,48},{80,96},{96,80},{112,128},{128,112... | collective-permute-start | bytes 638984 | tf_op jit(solution)/shard_map/ppermute | solution.py:351
  33.4 1.9 %collective-permute-start.3 = (bf16[2,208,256]{2,1,0:T(8,128)(2,1)S(1)}, bf16[2,208,256]{2,1,0:T(8,128)(2,1)S(1)}, u32[]{:S(2)}, u32[]{:S(2)}) collective-permute-start(bf16[2,208,256]{2,1,0:T(8,128)(2,1)S(1)} %get-tuple-element.14), channel_id=1, source_target_pairs={{0,16},{16,0},{32,48},{48,32},{64,80},{80,64},{96,112},{112,96},{1... | collective-permute-start | bytes 638984 | tf_op jit(solution)/shard_map/ppermute | solution.py:351
  35.3 0.0 copy-done.2
  35.3 0.0 copy-done.3
  35.3 0.0 copy-done.4
  35.3 0.0 copy-done.5
  35.3 0.0 copy-done.6
  35.3 0.0 copy-done.7
  35.3 0.0 copy-done.8
  35.4 0.0 copy-done.9
  35.4 0.0 copy-done.10
  35.4 0.0 copy-done.11
  35.4 8.7 %middle.1 = (bf16[1,16,96,256]{3,2,1,0:T(8,128)(2,1)}, bf16[3,4,96,256]{3,2,1,0:T(8,128)(2,1)S(1)}) custom-call(f32[32]{0:T(128)S(1)} %copy-done.8, f32[32]{0:T(128)S(1)} %copy-done.9, f32[32]{0:T(128)S(1)} %copy-done.10, f32[32]{0:T(128)S(1)} %copy-done.11, f32[1,256]{1,0:T(1,128)S(1)} %bitcast.5, f32[1,256]{1,0:T(1,128)S(1)} %bitcast.7, ...), custom_call_target="tpu_custom_call" | custom-call | tf_op jit(solution)/shard_map/middle/pallas_call | solution.py:220
  44.1 0.0 collective-permute-done.2.odd
  44.1 0.0 collective-permute-done.3.even
  44.1 5.0 %border.1 = bf16[1,16,96,256]{3,2,1,0:T(8,128)(2,1)} custom-call(f32[32]{0:T(128)S(1)} %copy-done.8, f32[32]{0:T(128)S(1)} %copy-done.9, f32[32]{0:T(128)S(1)} %copy-done.10, f32[32]{0:T(128)S(1)} %copy-done.11, f32[1,256]{1,0:T(1,128)S(1)} %bitcast.6, f32[1,256]{1,0:T(1,128)S(1)} %bitcast.8, ...), custom_call_target="tpu_custom_call", output_to_operand_aliasing={{}: (18, {})} | custom-call | tf_op jit(solution)/shard_map/border/pallas_call | solution.py:305
Async XLA Ops:
  0.0 20.6 %copy-start.1 = (bf16[1,16,96,256]{3,2,1,0:T(8,128)(2,1)S(1)}, bf16[1,16,96,256]{3,2,1,0:T(8,128)(2,1)}, u32[]{:S(2)}) copy-start(bf16[1,16,96,256]{3,2,1,0:T(8,128)(2,1)} %cot.7) | copy-start | bytes 2359300
  0.0 20.6 %copy-start = (bf16[1,16,96,256]{3,2,1,0:T(8,128)(2,1)S(1)}, bf16[1,16,96,256]{3,2,1,0:T(8,128)(2,1)}, u32[]{:S(2)}) copy-start(bf16[1,16,96,256]{3,2,1,0:T(8,128)(2,1)} %img.7) | copy-start | bytes 2359300
  1.1 34.2 %copy-start.2 = (bf16[3,3,256,256]{3,2,1,0:T(8,128)(2,1)S(1)}, bf16[3,3,256,256]{3,2,1,0:T(8,128)(2,1)}, u32[]{:S(2)}) copy-start(bf16[3,3,256,256]{3,2,1,0:T(8,128)(2,1)} %k1.3) | copy-start | bytes 3538948
  1.1 34.1 %copy-start.3 = (f32[256]{0:T(256)S(1)}, f32[256]{0:T(256)}, u32[]{:S(2)}) copy-start(f32[256]{0:T(256)} %param.16) | copy-start | bytes 3076
  1.2 34.1 %copy-start.4 = (f32[256]{0:T(256)S(1)}, f32[256]{0:T(256)}, u32[]{:S(2)}) copy-start(f32[256]{0:T(256)} %param.20) | copy-start | bytes 3076
  1.2 34.1 %copy-start.5 = (f32[256]{0:T(256)S(1)}, f32[256]{0:T(256)}, u32[]{:S(2)}) copy-start(f32[256]{0:T(256)} %param.21) | copy-start | bytes 3076
  1.2 34.1 %copy-start.6 = (f32[256]{0:T(256)S(1)}, f32[256]{0:T(256)}, u32[]{:S(2)}) copy-start(f32[256]{0:T(256)} %param.24) | copy-start | bytes 3076
  1.2 34.1 %copy-start.7 = (f32[256]{0:T(256)S(1)}, f32[256]{0:T(256)}, u32[]{:S(2)}) copy-start(f32[256]{0:T(256)} %param.25) | copy-start | bytes 3076
  1.2 34.1 %copy-start.8 = (f32[32]{0:T(128)S(1)}, f32[32]{0:T(128)}, u32[]{:S(2)}) copy-start(f32[32]{0:T(128)} %stats_0_.3) | copy-start | bytes 388
  1.2 34.1 %copy-start.9 = (f32[32]{0:T(128)S(1)}, f32[32]{0:T(128)}, u32[]{:S(2)}) copy-start(f32[32]{0:T(128)} %stats_1_.3) | copy-start | bytes 388
  1.2 34.1 %copy-start.10 = (f32[32]{0:T(128)S(1)}, f32[32]{0:T(128)}, u32[]{:S(2)}) copy-start(f32[32]{0:T(128)} %stats_2_.3) | copy-start | bytes 388
  1.2 34.1 %copy-start.11 = (f32[32]{0:T(128)S(1)}, f32[32]{0:T(128)}, u32[]{:S(2)}) copy-start(f32[32]{0:T(128)} %stats_3_.3) | copy-start | bytes 388
  1.3 17.7 %collective-permute-start = (bf16[2,32,256]{2,1,0:T(8,128)(2,1)S(1)}, bf16[2,32,256]{2,1,0:T(8,128)(2,1)S(1)}, u32[]{:S(2)}, u32[]{:S(2)}) collective-permute-start(bf16[2,32,256]{2,1,0:T(8,128)(2,1)S(1)} %get-tuple-element.11), channel_id=1, source_target_pairs={{0,1},{1,0},{2,3},{3,2},{4,5},{5,4},{6,7},{7,6},{8,9},{9,8},{10,11... | collective-permute-start | bytes 98312 | tf_op jit(solution)/shard_map/ppermute | solution.py:351
  4.0 16.6 %collective-permute-start.1 = (bf16[2,32,256]{2,1,0:T(8,128)(2,1)S(1)}, bf16[2,32,256]{2,1,0:T(8,128)(2,1)S(1)}, u32[]{:S(2)}, u32[]{:S(2)}) collective-permute-start(bf16[2,32,256]{2,1,0:T(8,128)(2,1)S(1)} %get-tuple-element.12), channel_id=1, source_target_pairs={{1,2},{2,1},{3,4},{4,3},{5,6},{6,5},{7,8},{8,7},{9,10},{10,9},{11,... | collective-permute-start | bytes 98312 | tf_op jit(solution)/shard_map/ppermute | solution.py:351
  20.6 23.4 %collective-permute-start.2 = (bf16[2,208,256]{2,1,0:T(8,128)(2,1)S(1)}, bf16[2,208,256]{2,1,0:T(8,128)(2,1)S(1)}, u32[]{:S(2)}, u32[]{:S(2)}) collective-permute-start(bf16[2,208,256]{2,1,0:T(8,128)(2,1)S(1)} %get-tuple-element.13), channel_id=1, source_target_pairs={{16,32},{32,16},{48,64},{64,48},{80,96},{96,80},{112,128},{128,112... | collective-permute-start | bytes 638984 | tf_op jit(solution)/shard_map/ppermute | solution.py:351
  33.4 10.7 %collective-permute-start.3 = (bf16[2,208,256]{2,1,0:T(8,128)(2,1)S(1)}, bf16[2,208,256]{2,1,0:T(8,128)(2,1)S(1)}, u32[]{:S(2)}, u32[]{:S(2)}) collective-permute-start(bf16[2,208,256]{2,1,0:T(8,128)(2,1)S(1)} %get-tuple-element.14), channel_id=1, source_target_pairs={{0,16},{16,0},{32,48},{48,32},{64,80},{80,64},{96,112},{112,96},{1... | collective-permute-start | bytes 638984 | tf_op jit(solution)/shard_map/ppermute | solution.py:351
